TPU v7x, 32 devices: a whole 2x2x4 slice. The times are simulated.
32 devices in a mesh: dp: 2 (over x), y: 4 (over z), x: 4 (over y, core).
Axes of the slice: x: 2, y: 2, z: 4, core: 2. Of those that a mesh axis runs over, the one named last changes fastest.
Arguments:
- tokens: int32 [3, 512], P(None, 'dp'), parts along dimension 1
- lengths: int32 [512], P('dp'), parts along dimension 0
- choices: int32 [3, 512, 8], P(None, 'dp'), parts along dimension 1
- emb_table: bfloat16 [49152, 1536], P(None, 'x')
- k_cache: bfloat16 [512, 256, 8, 64], P('dp', None, 'y'), parts along dimension 0
- v_cache: bfloat16 [512, 256, 8, 64], P('dp', None, 'y'), parts along dimension 0
- g_attn: bfloat16 [1536], P('x')
- w_q: bfloat16 [1536, 1536], P('x', 'y')
- w_k: bfloat16 [1536, 512], P('x', 'y')
- w_v: bfloat16 [1536, 512], P('x', 'y')
- w_o: bfloat16 [1536, 1536], P('y', 'x')
- g_ffn: bfloat16 [1536], P('x')
- w_router: bfloat16 [1536, 40], P('x')
- w_act: bfloat16 [40, 1536, 512], P(None, 'x', 'y')
- w_lin: bfloat16 [40, 1536, 512], P(None, 'x', 'y')
- w_down: bfloat16 [40, 512, 1536], P(None, 'y', 'x')
Outputs:
- output 1: bfloat16 [3, 512, 1536], P(None, 'dp', 'x'), parts along dimension 1
- output 2: bfloat16 [512, 256, 8, 64], P('dp', None, 'y'), parts along dimension 0
- output 3: bfloat16 [512, 256, 8, 64], P('dp', None, 'y'), parts along dimension 0
There are 2 independent parts. A program takes and returns all parts, laid end to end along the dimension named above; an argument that names none is the same for every part.
All inputs are finite; a program needn't handle non-finite values.
Results may differ from a plain program's by a relative error of at most 0.0115555.
Values are sent between devices in bfloat16 or wider.
A program may use at most 1 GiB of HBM per device.

v0:
```python
import jax
import jax.numpy as jnp
from jax import lax
from jax.sharding import PartitionSpec as P

EPS = 1e-5
ROPE_BASE = 1.0e6


def shard_norm(x_val, gain_vec, width_full):
    x_f32 = x_val.astype(jnp.float32)
    sq_total = lax.psum(jnp.sum(x_f32 * x_f32, axis=-1, keepdims=True), 'x')
    return (x_f32 * lax.rsqrt(sq_total / width_full + EPS) * gain_vec.astype(jnp.float32)).astype(jnp.bfloat16)


def rotate(vectors, positions):
    head_dim = vectors.shape[-1]
    half_dim = head_dim // 2
    inv_freq = ROPE_BASE ** (-(jnp.arange(half_dim, dtype=jnp.float32) * 2.0 / head_dim))
    angle_shape = (vectors.shape[0],) + (1,) * (vectors.ndim - 2) + (half_dim,)
    angles = (positions.astype(jnp.float32)[:, None] * inv_freq[None, :]).reshape(angle_shape)
    cosine = jnp.cos(angles)
    sine_val = jnp.sin(angles)
    first_half = vectors[..., :half_dim].astype(jnp.float32)
    second_half = vectors[..., half_dim:].astype(jnp.float32)
    return jnp.concatenate([first_half * cosine - second_half * sine_val, second_half * cosine + first_half * sine_val], axis=-1).astype(jnp.bfloat16)


def write_slot(cache_arr, new_rows, positions):
    hit_mask = (jnp.arange(cache_arr.shape[1])[None, :] == positions[:, None])[:, :, None, None]
    return jnp.where(hit_mask, new_rows[:, None], cache_arr)


def attention(queries, key_cache, val_cache, positions):
    head_dim = queries.shape[-1]
    scores = jnp.einsum('bkgh,bskh->bkgs', queries, key_cache, preferred_element_type=jnp.float32) * head_dim ** -0.5
    valid_mask = (jnp.arange(key_cache.shape[1])[None, :] <= positions[:, None])[:, None, None, :]
    scores = jnp.where(valid_mask, scores, -1.0e30)
    peak_val = jnp.max(scores, axis=-1, keepdims=True)
    weight = jnp.where(valid_mask, jnp.exp(scores - peak_val), 0.0)
    total_w = jnp.sum(weight, axis=-1, keepdims=True)
    mixed_out = jnp.einsum('bkgs,bskh->bkgh', weight.astype(jnp.bfloat16), val_cache, preferred_element_type=jnp.float32)
    return (mixed_out / total_w).astype(jnp.bfloat16)


def mixing(logits, choice_row, experts):
    gate_val = jax.nn.softmax(jnp.take_along_axis(logits, choice_row, axis=1), axis=-1)
    onehot = choice_row[:, :, None] == jnp.arange(experts)[None, None, :]
    return jnp.sum(jnp.where(onehot, gate_val[:, :, None], 0.0), axis=1)


def solution(mesh):
    x_count = mesh.shape['x']
    cache_spec = P('dp', None, 'y', None)
    in_specs = (P(None, 'dp'), P('dp'), P(None, 'dp', None), P(None, 'x'), cache_spec, cache_spec, P('x'), P('x', 'y'), P('x', 'y'), P('x', 'y'), P('y', 'x'), P('x'), P('x', None), P(None, 'x', 'y'), P(None, 'x', 'y'), P(None, 'y', 'x'))
    out_specs = (P(None, 'dp', 'x'), cache_spec, cache_spec)

    def per_device(tokens, lengths, choices, emb_table, k_cache, v_cache, g_attn, w_q, w_k, w_v, w_o, g_ffn, w_router, w_act, w_lin, w_down):
        n_batch = tokens.shape[1]
        kv_local, head_dim = k_cache.shape[2], k_cache.shape[3]
        q_cols = w_q.shape[1]
        kv_cols = w_k.shape[1]
        group_size = q_cols // head_dim // kv_local
        width_full = emb_table.shape[1] * x_count
        experts = w_act.shape[0]
        key_cache, val_cache = k_cache, v_cache
        step_outs = []
        for step_idx in range(tokens.shape[0]):
            positions = lengths + step_idx
            x_in = jnp.take(emb_table, tokens[step_idx], axis=0)
            normed = shard_norm(x_in, g_attn, width_full)
            proj_part = jnp.concatenate([jnp.dot(normed, w_q, preferred_element_type=jnp.float32), jnp.dot(normed, w_k, preferred_element_type=jnp.float32), jnp.dot(normed, w_v, preferred_element_type=jnp.float32)], axis=1).astype(jnp.bfloat16)
            proj_sum = lax.psum(proj_part, 'x')
            queries = rotate(proj_sum[:, :q_cols].reshape(n_batch, kv_local, group_size, head_dim), positions)
            new_keys = rotate(proj_sum[:, q_cols:q_cols + kv_cols].reshape(n_batch, kv_local, head_dim), positions)
            new_vals = proj_sum[:, q_cols + kv_cols:].reshape(n_batch, kv_local, head_dim)
            key_cache = write_slot(key_cache, new_keys, positions)
            val_cache = write_slot(val_cache, new_vals, positions)
            mixed = attention(queries, key_cache, val_cache, positions).reshape(n_batch, q_cols)
            attn_sum = lax.psum(jnp.dot(mixed, w_o, preferred_element_type=jnp.float32).astype(jnp.bfloat16), 'y')
            x_mid = (x_in.astype(jnp.float32) + attn_sum.astype(jnp.float32)).astype(jnp.bfloat16)
            normed2 = shard_norm(x_mid, g_ffn, width_full)
            logits = lax.psum(jnp.dot(normed2, w_router, preferred_element_type=jnp.float32), 'x')
            coef = mixing(logits, choices[step_idx], experts)
            hidden_part = jnp.stack([jnp.einsum('bd,edf->ebf', normed2, w_act, preferred_element_type=jnp.float32), jnp.einsum('bd,edf->ebf', normed2, w_lin, preferred_element_type=jnp.float32)]).astype(jnp.bfloat16)
            hidden_sum = lax.psum(hidden_part, 'x')
            unit_bf16 = (coef.T[:, :, None] * jax.nn.silu(hidden_sum[0].astype(jnp.float32)) * hidden_sum[1].astype(jnp.float32)).astype(jnp.bfloat16)
            moe_sum = lax.psum(jnp.einsum('ebf,efd->bd', unit_bf16, w_down, preferred_element_type=jnp.float32).astype(jnp.bfloat16), 'y')
            step_outs.append((x_mid.astype(jnp.float32) + moe_sum.astype(jnp.float32)).astype(jnp.bfloat16))
        return jnp.stack(step_outs), key_cache, val_cache

    return jax.shard_map(per_device, mesh=mesh, in_specs=in_specs, out_specs=out_specs, check_vma=False)
```

profile of v0, /device:TPU:0, one launch (start us, length us, event | category | flops | bytes accessed | tf_op | source)
XLA Modules:
  0.0 631.4 jit_solution(12105131784449526562)
XLA Ops:
  7.3 0.8 fusion.173
  8.2 2.7 gather_fusion.4
  10.9 2.7 gather_fusion.2
  13.6 2.7 gather_fusion
  16.9 8.4 %all-reduce.2 = (f32[256,1]{0,1:T(1,128)S(1)}, f32[256,1]{0,1:T(1,128)S(1)}, f32[256,1]{0,1:T(1,128)S(1)}) all-reduce(f32[256,1]{0,1:T(1,128)S(1)} %bitcast.258, f32[256,1]{0,1:T(1,128)S(1)} %bitcast.259, f32[256,1]{0,1:T(1,128)S(1)} %bitcast.260), channel_id=1, replica_groups=mesh['dp'=2,'y'=4,'x'=4] {'x'}, use_global_device_ids=true, to_apply=%region_29.32 | all-reduce | flops 768 | bytes 6144 | tf_op jit(solution)/shard_map/psum | solution.py:12
  26.5 0.3 convolution_convert_fusion.1
  26.9 0.3 convolution_convert_fusion.3
  27.8 0.3 convolution_convert_fusion.5
  28.1 0.8 pad_maximum_fusion.6
  28.9 0.8 pad_maximum_fusion.5
  29.6 0.8 pad_maximum_fusion.4
  30.7 0.4 multiply_cosine_fusion.2
  31.3 35.9 %all-reduce.17.cloned.1.call-done = (bf16[256,640]{1,0:T(8,128)(2,1)}, bf16[256,640]{1,0:T(8,128)(2,1)}, bf16[256,640]{1,0:T(8,128)(2,1)}) async-done(((bf16[256,640]{1,0:T(8,128)(2,1)}, bf16[256,640]{1,0:T(8,128)(2,1)}, bf16[256,640]{1,0:T(8,128)(2,1)}), (bf16[256,640]{1,0:T(8,128)(2,1)}, bf16[256,640]{1,0:T(8,128)(2,1)}, bf16[256,640]{1,0:T(8,128)(2,1)})) %all-reduce.17.cloned.1.call-update) | async-done | bytes 983056 | tf_op jit(solution)/shard_map/psum | solution.py:73
  67.2 0.9 fusion.172
  68.1 0.9 slice.162
  69.0 0.9 fusion.170
  69.9 0.9 slice.144
  70.9 0.9 fusion.171
  71.8 0.9 slice.153
  74.5 0.3 copy.163
  74.9 34.1 %broadcast_select_fusion.1 = (bf16[256,256,2,64]{1,3,2,0:T(8,128)(2,1)}, bf16[256,256,2,64]{1,3,2,0:T(8,128)(2,1)}) fusion(pred[256,256]{1,0:T(8,128)(4,1)S(1)} %get-tuple-element.81, bf16[256,256,2,64]{1,3,2,0:T(8,128)(2,1)} %param.24, pred[256,256]{1,0:T(8,128)(4,1)S(1)} %get-tuple-element.79, pred[256,256]{1,0:T(8,128)(4,1)S(1)} %get-tuple-element.97, ...), kind=kLoop, calls=%fused_computation.10 | loop fusion | flops 50331648 | bytes 67698688 | tf_op jit(solution)/shard_map/jit(_where)/select_n | solution.py:31
  108.9 8.4 %fusion.175 = (f32[256,2,3]{2,1,0:T(2,128)S(1)}, bf16[256,2,3,256]{3,2,1,0:T(4,128)(2,1)}) fusion(pred[256,256]{1,0:T(8,128)(4,1)S(1)} %get-tuple-element.80, bf16[256,2,3,64]{3,2,1,0:T(4,128)(2,1)S(1)} %copy.163, bf16[256,256,2,64]{1,3,2,0:T(8,128)(2,1)} %get-tuple-element.50), kind=kOutput, calls=%fused_computation.296 | convolution fusion | flops 52691200 | bytes 17831936 | tf_op jit(solution)/shard_map/sub | solution.py:40
  117.3 10.5 %fusion.39 = bf16[256,2,3,64]{3,2,1,0:T(4,128)(2,1)S(1)} fusion(bf16[256,256,2,64]{1,3,2,0:T(8,128)(2,1)} %get-tuple-element.51, bf16[256,2,3,256]{3,2,1,0:T(4,128)(2,1)} %get-tuple-element.92, f32[256,2,3]{2,1,0:T(2,128)S(1)} %get-tuple-element.91), kind=kOutput, calls=%fused_computation.76 | convolution fusion | flops 50528256 | bytes 17766400 | tf_op jit(solution)/shard_map/bkgs,bskh->bkgh/dot_general | solution.py:42
  128.6 0.3 copy.141
  129.0 12.4 %fusion.176 = (f32[256,2,3]{2,1,0:T(2,128)S(1)}, bf16[256,2,3,256]{3,2,1,0:T(4,128)(2,1)}) fusion(pred[256,256]{1,0:T(8,128)(4,1)S(1)} %get-tuple-element.78, bf16[256,2,3,64]{3,2,1,0:T(4,128)(2,1)S(1)} %copy.141, bf16[256,256,2,64]{1,3,2,0:T(8,128)(2,1)} %param.24, pred[256,256]{1,0:T(8,128)(4,1)S(1)} %get-tuple-element.79, bf16[256,2,64]{2,1,0:T(2,128)(2,1)S(1)} %copy.140), kind=kOutput, calls=%fused_computation.297 | convolution fusion | flops 61079808 | bytes 17963008 | tf_op jit(solution)/shard_map/sub | solution.py:40
  141.4 8.8 %divide_convert_fusion.1 = bf16[256,2,3,64]{3,2,1,0:T(4,128)(2,1)S(1)} fusion(bf16[256,256,2,64]{1,3,2,0:T(8,128)(2,1)} %param.25, pred[256,256]{1,0:T(8,128)(4,1)S(1)} %get-tuple-element.79, bf16[256,2,64]{2,1,0:T(2,128)(2,1)S(1)} %copy.143, bf16[256,2,3,256]{3,2,1,0:T(4,128)(2,1)} %get-tuple-element.94, f32[256,2,3]{2,1,0:T(2,128)S(1)} %get-tuple-element.93), kind=kOutput, calls=%fused_computation.103 | convolution fusion | flops 58916864 | bytes 17897472 | tf_op jit(solution)/shard_map/bkgs,bskh->bkgh/dot_general | solution.py:42
  150.5 1.0 convolution_convert_fusion
  151.5 1.0 convolution_convert_fusion.4
  152.8 14.4 %fusion.177 = (f32[256,2,3]{2,1,0:T(2,128)S(1)}, bf16[256,2,3,256]{3,2,1,0:T(4,128)(2,1)}) fusion(pred[256,256]{1,0:T(8,128)(4,1)S(1)} %get-tuple-element.98, bf16[256,2,3,64]{3,2,1,0:T(4,128)(2,1)S(1)} %copy.152, pred[256,256]{1,0:T(8,128)(4,1)S(1)} %get-tuple-element.97, bf16[256,256,2,64]{1,3,2,0:T(8,128)(2,1)} %param.24, ...), kind=kOutput, calls=%fused_computation.298 | convolution fusion | flops 69468416 | bytes 18094080 | tf_op jit(solution)/shard_map/sub | solution.py:40
  167.3 13.4 %divide_convert_fusion = bf16[256,2,3,64]{3,2,1,0:T(4,128)(2,1)S(1)} fusion(pred[256,256]{1,0:T(8,128)(4,1)S(1)} %get-tuple-element.97, bf16[256,256,2,64]{1,3,2,0:T(8,128)(2,1)} %param.25, pred[256,256]{1,0:T(8,128)(4,1)S(1)} %get-tuple-element.79, bf16[256,2,64]{2,1,0:T(2,128)(2,1)S(1)} %copy.154, bf16[256,2,64]{2,1,0:T(2,128)(2,1)S(1)} %copy.143, ...), kind=kOutput, calls=%fused_computation.102 | convolution fusion | flops 67305472 | bytes 18028544 | tf_op jit(solution)/shard_map/bkgs,bskh->bkgh/dot_general | solution.py:42
  180.9 1.0 convolution_convert_fusion.2
  182.0 40.3 %all-reduce.21.cloned.1.call-done = (bf16[256,384]{1,0:T(8,128)(2,1)}, bf16[256,384]{1,0:T(8,128)(2,1)}, bf16[256,384]{1,0:T(8,128)(2,1)}) async-done(((bf16[256,384]{1,0:T(8,128)(2,1)}, bf16[256,384]{1,0:T(8,128)(2,1)}, bf16[256,384]{1,0:T(8,128)(2,1)}), (bf16[256,384]{1,0:T(8,128)(2,1)}, bf16[256,384]{1,0:T(8,128)(2,1)}, bf16[256,384]{1,0:T(8,128)(2,1)})) %all-reduce.21.cloned.1.call-update) | async-done | bytes 589840 | tf_op jit(solution)/shard_map/psum | solution.py:80
  222.3 1.2 fusion.91
  223.5 1.2 fusion.75
  224.7 1.2 fusion.83
  226.0 5.7 all-reduce.1
  231.7 5.3 convert_bitcast_fusion
  237.0 3.1 convert_bitcast_fusion.1
  240.2 3.0 convert_bitcast_fusion.2
  243.2 3.0 convert_bitcast_fusion.3
  246.3 1.6 convert_bitcast_fusion.4
  247.9 3.1 convert_bitcast_fusion.5
  250.9 0.9 fusion.156
  251.8 0.9 fusion.148
  252.7 0.9 fusion.152
  253.6 5.5 pad_maximum_fusion.2
  259.1 2.8 pad_maximum_fusion.1
  262.0 4.5 pad_maximum_fusion
  266.5 0.7 copy-done.15
  267.9 25.7 %all-reduce.13.cloned.1.call-done = (f32[256,40]{0,1:T(8,128)}, f32[256,40]{0,1:T(8,128)}, f32[256,40]{0,1:T(8,128)}) async-done(((f32[256,40]{0,1:T(8,128)}, f32[256,40]{0,1:T(8,128)}, f32[256,40]{0,1:T(8,128)}), (f32[256,40]{0,1:T(8,128)}, f32[256,40]{0,1:T(8,128)}, f32[256,40]{0,1:T(8,128)})) %all-reduce.13.cloned.1.call-update) | async-done | bytes 122896 | tf_op jit(solution)/shard_map/psum | solution.py:83
  293.6 15.3 %gather_fusion.1 = f32[2048]{0:T(1024)S(1)} fusion(f32[256,40]{0,1:T(8,128)} %get-tuple-element.11, s32[2048]{0:T(1024)S(1)} %reshape.605), kind=kCustom, calls=%fused_computation.1.clone | custom fusion | bytes 32768 | tf_op jit(solution)/shard_map/jit(take_along_axis)/gather | solution.py:47
  309.1 0.6 copy-done.3
  309.7 16.8 %gather_fusion.5 = f32[2048]{0:T(1024)S(1)} fusion(f32[256,40]{0,1:T(8,128)S(1)} %copy-done.3, s32[2048]{0:T(1024)S(1)} %reshape.619), kind=kCustom, calls=%fused_computation.5.clone | custom fusion | bytes 32768 | tf_op jit(solution)/shard_map/jit(take_along_axis)/gather | solution.py:47
  326.7 0.6 copy-done.2
  327.3 16.8 %gather_fusion.3 = f32[2048]{0:T(1024)S(1)} fusion(f32[256,40]{0,1:T(8,128)S(1)} %copy-done.2, s32[2048]{0:T(1024)S(1)} %reshape.612), kind=kCustom, calls=%fused_computation.4.clone | custom fusion | bytes 32768 | tf_op jit(solution)/shard_map/jit(take_along_axis)/gather | solution.py:47
  344.5 223.1 %all-reduce.15.cloned.1.call-done = (bf16[2,40,256,128]{3,2,1,0:T(8,128)(2,1)}, bf16[2,40,256,128]{3,2,1,0:T(8,128)(2,1)}, bf16[2,40,256,128]{3,2,1,0:T(8,128)(2,1)}) async-done(((bf16[2,40,256,128]{3,2,1,0:T(8,128)(2,1)}, bf16[2,40,256,128]{3,2,1,0:T(8,128)(2,1)}, bf16[2,40,256,128]{3,2,1,0:T(8,128)(2,1)}), (bf16[2,40,256,128]{3,2,1,0:T(8,128)(2,1)}, bf16[2,40,256,128]{3,2,1,0:T(8,128)(2,1)}, ...) | async-done | bytes 15728656 | tf_op jit(solution)/shard_map/psum | solution.py:86
  567.6 6.1 fusion.55
  574.0 3.0 fusion.52
  577.0 3.0 fusion.49
  580.0 40.6 %all-reduce.19.cloned.1.call-done = (bf16[256,384]{1,0:T(8,128)(2,1)}, bf16[256,384]{1,0:T(8,128)(2,1)}, bf16[256,384]{1,0:T(8,128)(2,1)}) async-done(((bf16[256,384]{1,0:T(8,128)(2,1)}, bf16[256,384]{1,0:T(8,128)(2,1)}, bf16[256,384]{1,0:T(8,128)(2,1)}), (bf16[256,384]{1,0:T(8,128)(2,1)}, bf16[256,384]{1,0:T(8,128)(2,1)}, bf16[256,384]{1,0:T(8,128)(2,1)})) %all-reduce.19.cloned.1.call-update) | async-done | bytes 589840 | tf_op jit(solution)/shard_map/psum | solution.py:88
  620.6 1.0 fusion.107
  621.6 1.0 fusion.108
  622.6 1.0 fusion.109
  623.5 0.9 pad_maximum_fusion.3
  (139 shorter events, 8.1 us)
Async XLA Ops:
  7.2 19.3 %copy-start = (bf16[384,384]{1,0:T(8,128)(2,1)S(1)}, bf16[384,384]{1,0:T(8,128)(2,1)}, u32[]{:S(2)}) copy-start(bf16[384,384]{1,0:T(8,128)(2,1)} %param.27) | copy-start | bytes 884740
  7.2 18.1 %copy-start.17 = (bf16[384]{0:T(512)(128)(2,1)S(1)}, bf16[384]{0:T(512)(128)(2,1)}, u32[]{:S(2)}) copy-start(bf16[384]{0:T(512)(128)(2,1)} %param.26) | copy-start | bytes 2308
  7.2 18.1 %copy-start.21 = (bf16[384,128]{1,0:T(8,128)(2,1)S(1)}, bf16[384,128]{1,0:T(8,128)(2,1)}, u32[]{:S(2)}) copy-start(bf16[384,128]{1,0:T(8,128)(2,1)} %param.29) | copy-start | bytes 294916
  7.2 18.4 %copy-start.22 = (bf16[384,128]{1,0:T(8,128)(2,1)S(1)}, bf16[384,128]{1,0:T(8,128)(2,1)}, u32[]{:S(2)}) copy-start(bf16[384,128]{1,0:T(8,128)(2,1)} %param.28) | copy-start | bytes 294916
  7.2 60.0 %all-reduce.17.cloned.1.call-start = ((), (), s32[]{:S(2)}) async-start(), calls=%async_computation.2 | async-start | bytes 1966080 | tf_op jit(solution)/shard_map/psum | solution.py:73
  16.3 14.2 %copy-start.16 = (s32[256]{0:T(256)S(1)}, s32[256]{0:T(256)}, u32[]{:S(2)}) copy-start(s32[256]{0:T(256)} %param.21) | copy-start | bytes 3076
  30.4 191.9 %all-reduce.21.cloned.1.call-start = ((), (), s32[]{:S(2)}) async-start(), calls=%async_computation.4 | async-start | bytes 1179648 | tf_op jit(solution)/shard_map/psum | solution.py:80
  141.4 9.1 %copy-start.14 = (bf16[384,384]{1,0:T(8,128)(2,1)S(1)}, bf16[384,384]{1,0:T(8,128)(2,1)}, u32[]{:S(2)}) copy-start(bf16[384,384]{1,0:T(8,128)(2,1)} %param.30) | copy-start | bytes 884740
  167.2 14.8 %copy-start.18 = (bf16[384]{0:T(512)(128)(2,1)S(1)}, bf16[384]{0:T(512)(128)(2,1)}, u32[]{:S(2)}) copy-start(bf16[384]{0:T(512)(128)(2,1)} %param.31) | copy-start | bytes 2308
  181.9 111.7 %all-reduce.13.cloned.1.call-start = ((), (), s32[]{:S(2)}) async-start(), calls=%async_computation | async-start | bytes 245760 | tf_op jit(solution)/shard_map/psum | solution.py:83
  223.5 28.4 %copy-start.10 = (bf16[256,384]{1,0:T(8,128)(2,1)}, bf16[256,384]{1,0:T(8,128)(2,1)S(1)}, u32[]{:S(2)}) copy-start(bf16[256,384]{1,0:T(8,128)(2,1)S(1)} %get-tuple-element.37) | copy-start | bytes 589828
  224.7 26.2 %copy-start.8 = (bf16[256,384]{1,0:T(8,128)(2,1)}, bf16[256,384]{1,0:T(8,128)(2,1)S(1)}, u32[]{:S(2)}) copy-start(bf16[256,384]{1,0:T(8,128)(2,1)S(1)} %get-tuple-element.35) | copy-start | bytes 589828
  226.0 26.8 %copy-start.12 = (bf16[256,384]{1,0:T(8,128)(2,1)}, bf16[256,384]{1,0:T(8,128)(2,1)S(1)}, u32[]{:S(2)}) copy-start(bf16[256,384]{1,0:T(8,128)(2,1)S(1)} %get-tuple-element.33) | copy-start | bytes 589828
  231.6 5.4 copy-start.5
  237.0 3.2 copy-start.4
  247.8 3.1 copy-start.23
  253.6 5.5 copy-start.6
  253.6 5.5 copy-start.7
  261.9 305.7 %all-reduce.15.cloned.1.call-start = ((), (), s32[]{:S(2)}) async-start(), calls=%async_computation.1 | async-start | bytes 31457280 | tf_op jit(solution)/shard_map/psum | solution.py:86
  266.4 0.7 copy-start.15
  266.4 354.1 %all-reduce.19.cloned.1.call-start = ((), (), s32[]{:S(2)}) async-start(), calls=%async_computation.3 | async-start | bytes 1179648 | tf_op jit(solution)/shard_map/psum | solution.py:88
  309.0 0.8 copy-start.3
  326.5 0.8 copy-start.2
  567.6 6.1 copy-start.19
  567.6 6.4 %copy-start.20 = (bf16[40,128,384]{2,1,0:T(8,128)(2,1)S(1)}, bf16[40,128,384]{2,1,0:T(8,128)(2,1)}, u32[]{:S(2)}) copy-start(bf16[40,128,384]{2,1,0:T(8,128)(2,1)} %param.35) | copy-start | bytes 11796484
  567.6 9.4 %slice-start = ((s8[5242880]{0:T(1024)(128)(4,1)}), s8[4194304]{0:T(1024)(128)(4,1)S(1)}, s32[]{:S(2)}) async-start(s8[5242880]{0:T(1024)(128)(4,1)} %bitcast.276), calls=%async_computation.5 | async-start | bytes 8388608
  574.0 3.0 slice-start.1
  576.9 43.6 %copy-start.11 = (bf16[256,384]{1,0:T(8,128)(2,1)S(1)}, bf16[256,384]{1,0:T(8,128)(2,1)}, u32[]{:S(2)}) copy-start(bf16[256,384]{1,0:T(8,128)(2,1)} %copy-done.10) | copy-start | bytes 589828
  576.9 44.6 %copy-start.13 = (bf16[256,384]{1,0:T(8,128)(2,1)S(1)}, bf16[256,384]{1,0:T(8,128)(2,1)}, u32[]{:S(2)}) copy-start(bf16[256,384]{1,0:T(8,128)(2,1)} %copy-done.12) | copy-start | bytes 589828
  577.0 45.6 %copy-start.9 = (bf16[256,384]{1,0:T(8,128)(2,1)S(1)}, bf16[256,384]{1,0:T(8,128)(2,1)}, u32[]{:S(2)}) copy-start(bf16[256,384]{1,0:T(8,128)(2,1)} %copy-done.8) | copy-start | bytes 589828
  577.0 47.5 %copy-start.1 = (bf16[384,384]{1,0:T(8,128)(2,1)S(1)}, bf16[384,384]{1,0:T(8,128)(2,1)}, u32[]{:S(2)}) copy-start(bf16[384,384]{1,0:T(8,128)(2,1)} %param.27) | copy-start | bytes 884740
Sparse Core Ops, SparseCore 0:
  30.5 36.6 all-reduce.16
  182.1 40.1 all-reduce.20
  262.0 31.5 all-reduce.12
  296.2 271.3 all-reduce.14
  580.1 40.4 all-reduce.18
where the time goes:
time: 639 us; the launch traced here: 631 us
  waiting for transfers between devices  366 us (57%)
  matrix products  107 us (17%)
  local copies, waits for them, and re-layouts  70.3 us (11%)
  other arithmetic  58.6 us (9%)
  between operations  15 us (2%)
  blocking collectives  14.1 us (2%)
    psum x1, waiting for transfers between devices, per_device(): hidden_sum = lax.psum(hidden_part, 'x')  223 us
    gather x15, local copies, waits for them, and re-layouts, mixing(): jnp.take_along_axis(logits, choice_row, axis=1)  50 us
    psum x1, waiting for transfers between devices, per_device(): lax.psum(jnp.einsum('ebf,efd->bd', unit_bf16, w_down, preferred_element_t...  40.6 us
    psum x1, waiting for transfers between devices, per_device(): lax.psum(jnp.dot(mixed, w_o, preferred_element_type=jnp.float32).astype(j...  40.3 us
    psum x1, waiting for transfers between devices, per_device(): proj_sum = lax.psum(proj_part, 'x')  35.9 us
    sub x3, matrix products, attention(): weight = jnp.where(valid_mask, jnp.exp(scores - peak_val), 0.0)  35.2 us
    select_n x1, other arithmetic, write_slot(): return jnp.where(hit_mask, new_rows[:, None], cache_arr)  34.1 us
    dot_general x3, matrix products, attention(): jnp.einsum('bkgs,bskh->bkgh', weight.astype(jnp.bfloat16), val_cache, pre...  32.7 us
  transfers between devices with their start and end apart: 5, of which 5 were waited for; matrix products, arithmetic and copies ran while one was open for 9% of the time, Pallas kernels for 0%

commit v1 on v0

v1 whole, which is shorter than its diff:
```python
import functools
import jax
import jax.numpy as jnp
from jax import lax
from jax.experimental import pallas as pl
from jax.experimental.pallas import tpu as pltpu
from jax.sharding import PartitionSpec as P

EPS = 1e-5
ROPE_BASE = 1.0e6
MESH = pl.DeviceIdType.MESH
F32 = jnp.float32
BF16 = jnp.bfloat16
NB = 8
QROWS = 16


def attn_body(len_ref, q_ref, kn_ref, vn_ref, k_ref, v_ref, o_ref, ko_ref, vo_ref, *, steps, group):
    seq = k_ref.shape[2]
    step = pl.program_id(0)
    knt = kn_ref[0].astype(F32).T.astype(BF16)
    vnt = vn_ref[0].astype(F32).T.astype(BF16)
    new_t = jnp.concatenate([knt, vnt], axis=0)
    n_new = new_t.shape[1]
    row_id = lax.broadcasted_iota(jnp.int32, (n_new, seq), 0)
    col_id = lax.broadcasted_iota(jnp.int32, (n_new, seq), 1)
    lane1 = lax.broadcasted_iota(jnp.int32, (1, seq), 1)
    srow = lax.broadcasted_iota(jnp.int32, (2 * QROWS, seq), 0)
    scol = lax.broadcasted_iota(jnp.int32, (2 * QROWS, seq), 1)
    srow = jnp.where(srow >= QROWS, srow - QROWS, srow)
    t_of = jnp.where(srow >= 2 * group, 2, jnp.where(srow >= group, 1, 0))
    rel = scol - t_of
    low = lax.broadcasted_iota(jnp.int32, (QROWS, 128), 1) < 64
    half = k_ref.shape[1]
    for b in range(NB):
        pos = len_ref[step * NB + b]
        place = jnp.where(row_id - b * steps == col_id - pos, 1.0, 0.0)
        place = jnp.where((row_id >= b * steps) & (row_id < (b + 1) * steps), place, 0.0).astype(BF16)
        placed = jnp.dot(new_t, place, preferred_element_type=F32).astype(BF16)
        hit = jnp.broadcast_to((lane1 >= pos) & (lane1 < pos + steps), (half, seq))
        k_new = jnp.where(hit, placed[:half], k_ref[b])
        v_new = jnp.where(hit, placed[half:], v_ref[b])
        ko_ref[b] = k_new
        vo_ref[b] = v_new
        q16 = q_ref[b]
        zero = jnp.zeros_like(q16)
        q32 = jnp.concatenate([jnp.where(low, q16, zero), jnp.where(low, zero, q16)], axis=0)
        s = jnp.dot(q32, k_new, preferred_element_type=F32) * 0.125
        ok = rel <= pos
        s = jnp.where(ok, s, -1.0e30)
        peak = jnp.max(s, axis=1, keepdims=True)
        w = jnp.where(ok, jnp.exp(s - peak), 0.0)
        tot = jnp.sum(w, axis=1, keepdims=True)
        o = lax.dot_general(w.astype(BF16), v_new, (((1,), (1,)), ((), ())), preferred_element_type=F32)
        o = o / tot
        o_ref[b] = jnp.where(low, o[:QROWS], o[QROWS:]).astype(BF16)


def attention(lengths, q, kn, vn, kc, vc, steps, group):
    nb, half, seq = kc.shape
    grid = nb // NB
    cache = pl.BlockSpec((NB, half, seq), lambda i, l: (i, 0, 0))
    new = pl.BlockSpec((1,) + kn.shape[1:], lambda i, l: (i, 0, 0))
    qs = pl.BlockSpec((NB, QROWS, 128), lambda i, l: (i, 0, 0))
    return pl.pallas_call(
        functools.partial(attn_body, steps=steps, group=group),
        grid_spec=pltpu.PrefetchScalarGridSpec(num_scalar_prefetch=1, grid=(grid,), in_specs=[qs, new, new, cache, cache], out_specs=[qs, cache, cache]),
        out_shape=[jax.ShapeDtypeStruct((nb, QROWS, 128), BF16), jax.ShapeDtypeStruct(kc.shape, BF16), jax.ShapeDtypeStruct(vc.shape, BF16)],
        compiler_params=pltpu.CompilerParams(vmem_limit_bytes=40 * 1024 * 1024, dimension_semantics=("arbitrary",)),
        cost_estimate=pl.CostEstimate(flops=2 * nb * 32 * 128 * seq * 2, bytes_accessed=4 * nb * half * seq * 2, transcendentals=0),
    )(lengths, q, kn, vn, kc, vc)


def moe_body(h_ref, xm_ref, wr_ref, chb_ref, wact_hbm, wlin_hbm, wdn_hbm, out_ref,
             wcat, wdn, hd, hs, rs1, cs, rs2, lgp, lr1, lcs, lr2, u, ud, pd, yr,
             wsem, s1s, s1r, s2s, s2r, ls, lr, us, ur, ys, yrs, gs, gr):
    experts = wcat.shape[0]
    ff = wact_hbm.shape[2]
    steps = hs.shape[0]
    nb = hs.shape[1]
    hb, qb = nb // 2, nb // 4
    top = chb_ref.shape[0]
    dp, y, x = lax.axis_index("dp"), lax.axis_index("y"), lax.axis_index("x")
    core, chip = x % 2, x // 2
    sib = (dp, y, chip * 2 + (1 - core))
    peer = (dp, y, (1 - chip) * 2 + core)
    ypeer = [None] + [(dp, (y + d) % 4, x) for d in (1, 2, 3)]

    def rcopy(src, dst, ssem, rsem, dev):
        return pltpu.make_async_remote_copy(src_ref=src, dst_ref=dst, send_sem=ssem, recv_sem=rsem, device_id=dev, device_id_type=MESH)

    w0 = pltpu.make_async_copy(wact_hbm, wcat.at[:, :, pl.ds(0, ff)], wsem.at[0])
    w1 = pltpu.make_async_copy(wlin_hbm, wcat.at[:, :, pl.ds(ff, ff)], wsem.at[1])
    w2 = pltpu.make_async_copy(wdn_hbm, wdn, wsem.at[2])
    w0.start()
    w1.start()
    w2.start()

    barrier = pltpu.get_barrier_semaphore()
    for dev in [sib, peer] + ypeer[1:]:
        pl.semaphore_signal(barrier, inc=1, device_id=dev, device_id_type=MESH)
    lg = jnp.dot(h_ref[...], wr_ref[...], preferred_element_type=F32)
    for c in range(steps):
        lgp[c] = lg[c * nb:(c + 1) * nb]
    pl.semaphore_wait(barrier, 5)

    keep = pl.multiple_of(core * hb, hb)
    give = pl.multiple_of((1 - core) * hb, hb)
    sub_keep = pl.multiple_of(chip * qb, qb)
    sub_give = pl.multiple_of((1 - chip) * qb, qb)
    own = pl.multiple_of(core * hb + chip * qb, qb)
    other = pl.multiple_of(core * hb + (1 - chip) * qb, qb)
    sib_own = pl.multiple_of((1 - core) * hb + chip * qb, qb)
    sib_other = pl.multiple_of((1 - core) * hb + (1 - chip) * qb, qb)

    l1 = rcopy(lgp.at[:, pl.ds(give, hb), :], lr1, ls.at[0], lr.at[0], sib)
    l1.start()

    def part_a(c):
        def one(e, carry):
            hd[e] = jnp.dot(h_ref[c * nb:(c + 1) * nb, :], wcat[e], preferred_element_type=F32).astype(BF16)
            return carry
        lax.fori_loop(0, experts, one, 0)

        def pick(i, carry):
            r = pl.multiple_of(i * 16, 16)
            ch = [chb_ref[j, pl.ds(pl.multiple_of(c * nb + i * 16, 16), 16), :] for j in range(top)]
            acc_a = [jnp.zeros((16, ff), BF16) for _ in range(top)]
            acc_l = [jnp.zeros((16, ff), BF16) for _ in range(top)]
            for e in range(experts):
                va = hd[e, pl.ds(r, 16), 0:ff]
                vl = hd[e, pl.ds(r, 16), ff:2 * ff]
                for j in range(top):
                    m = ch[j] == jnp.asarray(e, BF16)
                    acc_a[j] = jnp.where(m, va, acc_a[j])
                    acc_l[j] = jnp.where(m, vl, acc_l[j])
            for j in range(top):
                hs[c, pl.ds(r, 16), 2 * j * ff:(2 * j + 1) * ff] = acc_a[j]
                hs[c, pl.ds(r, 16), (2 * j + 1) * ff:(2 * j + 2) * ff] = acc_l[j]
            return carry
        lax.fori_loop(0, nb // 16, pick, 0)

    def s1(c):
        return rcopy(hs.at[c, pl.ds(give, hb), :], rs1.at[c], s1s.at[c], s1r.at[c], sib)

    def s2(c):
        return rcopy(cs.at[c], rs2.at[c], s2s.at[c], s2r.at[c], peer)

    def part_b(c):
        s1(c).wait_recv()

        def add(i, carry):
            r = pl.multiple_of(i * 16, 16)
            mine = hs[c, pl.ds(pl.multiple_of(keep + sub_give + r, 16), 16), :].astype(F32)
            got = rs1[c, pl.ds(pl.multiple_of(sub_give + r, 16), 16), :].astype(F32)
            cs[c, pl.ds(r, 16), :] = (mine + got).astype(BF16)
            return carry
        lax.fori_loop(0, qb // 16, add, 0)
        s2(c).start()

    def u_peer(c, row):
        return rcopy(u.at[c, pl.ds(row, qb), :], u.at[c, pl.ds(row, qb), :], us.at[c, 0], ur.at[c, 0], peer)

    def u_sib(c, row, k):
        return rcopy(u.at[c, pl.ds(row, qb), :], u.at[c, pl.ds(row, qb), :], us.at[c, k], ur.at[c, k], sib)

    def part_u(c):
        s2(c).wait_recv()

        def tile(i, carry):
            r = pl.multiple_of(i * 16, 16)
            r_own = pl.multiple_of(own + r, 16)
            r_sub = pl.multiple_of(sub_keep + r, 16)
            logit = lgp[c, pl.ds(r_own, 16), :] + lr1[c, pl.ds(r_sub, 16), :] + lr2[c, pl.ds(r, 16), :]
            lane = lax.broadcasted_iota(jnp.int32, (16, 128), 1).astype(F32)
            hit = [chb_ref[j, pl.ds(pl.multiple_of(c * nb + own + r, 16), 16), :].astype(F32) == lane for j in range(top)]
            any_hit = hit[0]
            for j in range(1, top):
                any_hit = any_hit | hit[j]
            peak = jnp.max(jnp.where(any_hit, logit, -jnp.inf), axis=1, keepdims=True)
            ex = jnp.where(any_hit, jnp.exp(logit - peak), 0.0)
            coef = ex / jnp.sum(ex, axis=1, keepdims=True)
            for j in range(top):
                gate = jnp.sum(jnp.where(hit[j], coef, 0.0), axis=1, keepdims=True)
                ca, cl = pl.ds(2 * j * ff, ff), pl.ds((2 * j + 1) * ff, ff)
                act = hs[c, pl.ds(r_own, 16), ca].astype(F32) + rs1[c, pl.ds(r_sub, 16), ca].astype(F32) + rs2[c, pl.ds(r, 16), ca].astype(F32)
                lin = hs[c, pl.ds(r_own, 16), cl].astype(F32) + rs1[c, pl.ds(r_sub, 16), cl].astype(F32) + rs2[c, pl.ds(r, 16), cl].astype(F32)
                val = gate * (act / (1.0 + jnp.exp(-act))) * lin
                u[c, pl.ds(r_own, 16), j * ff:(j + 1) * ff] = val.astype(BF16)
            return carry
        lax.fori_loop(0, qb // 16, tile, 0)
        u_peer(c, own).start()
        u_sib(c, own, 1).start()

    def part_f(c):
        u_peer(c, other).wait_recv()
        u_sib(c, other, 2).start()

    def y_rs(c, d):
        row = pl.multiple_of(((y + d) % 4) * qb, qb)
        return rcopy(pd.at[c, pl.ds(row, qb), :], yr.at[c, 3 - d], ys.at[c, d - 1], yrs.at[c, 3 - d], ypeer[d])

    def y_rs_recv(c, k):
        return rcopy(pd.at[c, pl.ds(0, qb), :], yr.at[c, k], ys.at[c, k], yrs.at[c, k], ypeer[1])

    def part_d(c):
        u_sib(c, sib_own, 1).wait_recv()
        u_sib(c, sib_other, 2).wait_recv()

        def spread(i, carry):
            r = pl.multiple_of(i * 16, 16)
            ch = [chb_ref[j, pl.ds(pl.multiple_of(c * nb + i * 16, 16), 16), :] for j in range(top)]
            vals = [u[c, pl.ds(r, 16), j * ff:(j + 1) * ff] for j in range(top)]
            for e in range(experts):
                acc = jnp.zeros((16, ff), BF16)
                for j in range(top):
                    acc = jnp.where(ch[j] == jnp.asarray(e, BF16), vals[j], acc)
                ud[pl.ds(r, 16), e * ff:(e + 1) * ff] = acc
            return carry
        lax.fori_loop(0, nb // 16, spread, 0)
        pd[c] = jnp.dot(ud[...], wdn[...], preferred_element_type=F32).astype(BF16)
        for d in (1, 2, 3):
            y_rs(c, d).start()

    def y_ag(c, d):
        row = pl.multiple_of(y * qb, qb)
        return rcopy(out_ref.at[c, pl.ds(row, qb), :], out_ref.at[c, pl.ds(row, qb), :], gs.at[c, d - 1], gr.at[c, 3 - d], ypeer[d])

    def y_ag_recv(c, k):
        row = pl.multiple_of(((y + k + 1) % 4) * qb, qb)
        return rcopy(out_ref.at[c, pl.ds(row, qb), :], out_ref.at[c, pl.ds(row, qb), :], gs.at[c, k], gr.at[c, k], ypeer[1])

    def part_g(c):
        for k in range(3):
            y_rs_recv(c, k).wait_recv()
        row = pl.multiple_of(y * qb, qb)
        tot = xm_ref[pl.ds(pl.multiple_of(c * nb + y * qb, qb), qb), :].astype(F32)
        acc = pd[c, pl.ds(row, qb), :].astype(F32)
        for k in range(3):
            acc = acc + yr[c, k].astype(F32)
        out_ref[c, pl.ds(row, qb), :] = (tot + acc).astype(BF16)
        for d in (1, 2, 3):
            y_ag(c, d).start()

    w0.wait()
    w1.wait()
    part_a(0)
    s1(0).start()
    l1.wait_recv()
    lcs[...] = lgp[:, pl.ds(pl.multiple_of(keep + sub_give, qb), qb), :] + lr1[:, pl.ds(sub_give, qb), :]
    l2 = rcopy(lcs, lr2, ls.at[1], lr.at[1], peer)
    l2.start()
    part_b(0)
    part_a(1)
    s1(1).start()
    l2.wait_recv()
    part_u(0)
    part_b(1)
    part_a(2)
    s1(2).start()
    part_f(0)
    part_u(1)
    part_b(2)
    w2.wait()
    part_d(0)
    part_f(1)
    part_d(1)
    part_u(2)
    part_g(0)
    part_g(1)
    part_f(2)
    part_d(2)
    part_g(2)
    for c in range(steps):
        for k in range(3):
            y_ag_recv(c, k).wait_recv()
    l1.wait_send()
    l2.wait_send()
    for c in range(steps):
        s1(c).wait_send()
        s2(c).wait_send()
        u_peer(c, own).wait_send()
        u_sib(c, own, 1).wait_send()
        u_sib(c, other, 2).wait_send()
        for d in (1, 2, 3):
            y_rs(c, d).wait_send()
            y_ag(c, d).wait_send()


def moe(h2, x_mid, w_router, chb, w_act, w_lin, w_down, steps):
    rows, width = h2.shape
    nb = rows // steps
    experts, _, ff = w_act.shape
    top = chb.shape[0]
    hb, qb = nb // 2, nb // 4
    dma = pltpu.SemaphoreType.DMA
    vm = pl.BlockSpec(memory_space=pltpu.VMEM)
    hbm = pl.BlockSpec(memory_space=pl.ANY)
    return pl.pallas_call(
        moe_body,
        out_shape=jax.ShapeDtypeStruct((steps, nb, width), BF16),
        in_specs=[vm, vm, vm, vm, hbm, hbm, hbm],
        out_specs=vm,
        scratch_shapes=[
            pltpu.VMEM((experts, width, 2 * ff), BF16),
            pltpu.VMEM((experts * ff, width), BF16),
            pltpu.VMEM((experts, nb, 2 * ff), BF16),
            pltpu.VMEM((steps, nb, 2 * top * ff), BF16),
            pltpu.VMEM((steps, hb, 2 * top * ff), BF16),
            pltpu.VMEM((steps, qb, 2 * top * ff), BF16),
            pltpu.VMEM((steps, qb, 2 * top * ff), BF16),
            pltpu.VMEM((steps, nb, 128), F32),
            pltpu.VMEM((steps, hb, 128), F32),
            pltpu.VMEM((steps, qb, 128), F32),
            pltpu.VMEM((steps, qb, 128), F32),
            pltpu.VMEM((steps, nb, top * ff), BF16),
            pltpu.VMEM((nb, experts * ff), BF16),
            pltpu.VMEM((steps, nb, width), BF16),
            pltpu.VMEM((steps, 3, qb, width), BF16),
            dma((3,)), dma((steps,)), dma((steps,)), dma((steps,)), dma((steps,)),
            dma((2,)), dma((2,)), dma((steps, 3)), dma((steps, 3)),
            dma((steps, 3)), dma((steps, 3)), dma((steps, 3)), dma((steps, 3)),
        ],
        compiler_params=pltpu.CompilerParams(collective_id=1, has_side_effects=True, vmem_limit_bytes=56 * 1024 * 1024),
        cost_estimate=pl.CostEstimate(flops=6 * rows * width * experts * ff, bytes_accessed=12 * 1024 * 1024, transcendentals=0),
    )(h2, x_mid, w_router, chb, w_act, w_lin, w_down.reshape(experts * ff, width))


def shard_norm(x_val, gain_vec, width_full):
    x_f32 = x_val.astype(F32)
    sq_total = lax.psum(jnp.sum(x_f32 * x_f32, axis=-1, keepdims=True), 'x')
    return (x_f32 * lax.rsqrt(sq_total / width_full + EPS) * gain_vec.astype(F32)).astype(BF16)


def rotate(vectors, positions):
    head_dim = vectors.shape[-1]
    half_dim = head_dim // 2
    inv_freq = ROPE_BASE ** (-(jnp.arange(half_dim, dtype=F32) * 2.0 / head_dim))
    angle_shape = (vectors.shape[0],) + (1,) * (vectors.ndim - 2) + (half_dim,)
    angles = (positions.astype(F32)[:, None] * inv_freq[None, :]).reshape(angle_shape)
    cosine = jnp.cos(angles)
    sine_val = jnp.sin(angles)
    first_half = vectors[..., :half_dim].astype(F32)
    second_half = vectors[..., half_dim:].astype(F32)
    return jnp.concatenate([first_half * cosine - second_half * sine_val, second_half * cosine + first_half * sine_val], axis=-1).astype(BF16)


def solution(mesh):
    x_count = mesh.shape['x']
    cache_spec = P('dp', None, 'y', None)
    in_specs = (P(None, 'dp'), P('dp'), P(None, 'dp', None), P(None, 'x'), cache_spec, cache_spec, P('x'), P('x', 'y'), P('x', 'y'), P('x', 'y'), P('y', 'x'), P('x'), P('x', None), P(None, 'x', 'y'), P(None, 'x', 'y'), P(None, 'y', 'x'))
    out_specs = (P(None, 'dp', 'x'), cache_spec, cache_spec)

    def per_device(tokens, lengths, choices, emb_table, k_cache, v_cache, g_attn, w_q, w_k, w_v, w_o, g_ffn, w_router, w_act, w_lin, w_down):
        steps, nb = tokens.shape
        seq, kvl, hdim = k_cache.shape[1:]
        q_cols, kv_cols = w_q.shape[1], w_k.shape[1]
        width = emb_table.shape[1]
        width_full = width * x_count
        group = q_cols // kv_cols
        rows = steps * nb
        top = choices.shape[2]
        positions = (lengths[None, :] + jnp.arange(steps, dtype=lengths.dtype)[:, None]).reshape(rows)
        wq = w_q.reshape(width, kvl, group, hdim).transpose(0, 2, 1, 3).reshape(width, q_cols)
        wo = w_o.reshape(kvl, group, hdim, width).transpose(1, 0, 2, 3).reshape(q_cols, width)
        w_all = jnp.concatenate([wq, w_k, w_v], axis=1)
        chb = jnp.broadcast_to(choices.reshape(rows, top).T.astype(BF16)[:, :, None], (top, rows, 128))
        wr = jnp.pad(w_router, ((0, 0), (0, 128 - w_router.shape[1])))

        x_in = jnp.take(emb_table, tokens.reshape(rows), axis=0)
        normed = shard_norm(x_in, g_attn, width_full)
        proj = lax.psum(jnp.dot(normed, w_all, preferred_element_type=F32).astype(BF16), 'x')
        heads = q_cols // hdim
        qk = rotate(proj[:, :q_cols + kv_cols].reshape(rows, heads + kvl, hdim), positions)
        q = qk[:, :heads].reshape(steps, nb, group, kvl * hdim).transpose(1, 0, 2, 3).reshape(nb, steps * group, kvl * hdim)
        q = jnp.pad(q, ((0, 0), (0, QROWS - steps * group), (0, 0)))
        kn = qk[:, heads:].reshape(steps, nb, kv_cols).transpose(1, 0, 2).reshape(nb // NB, NB * steps, kv_cols)
        vn = proj[:, q_cols + kv_cols:].reshape(steps, nb, kv_cols).transpose(1, 0, 2).reshape(nb // NB, NB * steps, kv_cols)
        pad = 32 - NB * steps
        kn = jnp.pad(kn, ((0, 0), (0, pad), (0, 0)))
        vn = jnp.pad(vn, ((0, 0), (0, pad), (0, 0)))
        kc = k_cache.transpose(0, 2, 3, 1).reshape(nb, kv_cols, seq)
        vc = v_cache.transpose(0, 2, 3, 1).reshape(nb, kv_cols, seq)
        o, ko, vo = attention(lengths, q, kn, vn, kc, vc, steps, group)
        mixed = o[:, :steps * group].reshape(nb, steps, q_cols).transpose(1, 0, 2).reshape(rows, q_cols)
        attn = lax.psum(jnp.dot(mixed, wo, preferred_element_type=F32).astype(BF16), 'y')
        x_mid = (x_in.astype(F32) + attn.astype(F32)).astype(BF16)
        h2 = shard_norm(x_mid, g_ffn, width_full)
        hidden = moe(h2, x_mid, wr, chb, w_act, w_lin, w_down, steps)
        ko = ko.reshape(nb, kvl, hdim, seq).transpose(0, 3, 1, 2)
        vo = vo.reshape(nb, kvl, hdim, seq).transpose(0, 3, 1, 2)
        return hidden, ko, vo

    return jax.shard_map(per_device, mesh=mesh, in_specs=in_specs, out_specs=out_specs, check_vma=False)
```

time: 639 us -> 324 us (0.51); the launches traced: 631 us -> 324 us
  waiting for transfers between devices: 366 us -> 73.7 us
  Pallas kernels: 0 us -> 195 us
  matrix products: 107 us -> 3.09 us
  other arithmetic: 58.6 us -> 3.77 us
  local copies, waits for them, and re-layouts: 70.3 us -> 19.6 us
    psum x5 -> x2, waiting for transfers between devices: 366 us -> 73.6 us  [the longest x1 39.3 us: per_device(): lax.psum(jnp.dot(mixed, wo, preferred_element_type=F32).astype(BF16), 'y')]
    pallas_call x0 -> x2, Pallas kernels: none -> 195 us  [the longest x1 101 us: attention(): pl.pallas_call(functools.partial(attn_body, steps=steps, group=group), gr...]
    dot_general x27 -> x2, matrix products: 72.2 us -> 3.09 us  [the longest x1 1.76 us: per_device(): jnp.dot(normed, w_all, preferred_element_type=F32).astype(BF16)]
    gather x18 -> x1, local copies, waits for them, and re-layouts: 58.1 us -> 5.01 us  [per_device(): x_in = jnp.take(emb_table, tokens.reshape(rows), axis=0)]
    sub x3 -> x0, matrix products: 35.2 us -> none  [attention(): weight = jnp.where(valid_mask, jnp.exp(scores - peak_val), 0.0)]
    select_n x4 -> x1, other arithmetic: 34.1 us -> 0.02 us  [per_device(): x_in = jnp.take(emb_table, tokens.reshape(rows), axis=0)]
    another operation x11 -> x1, other arithmetic: 16.8 us -> 0.24 us  [the longest x3 12.7 us: per_device(): jnp.stack([jnp.einsum('bd,edf->ebf', normed2, w_act, preferred_element_ty...]
  transfers between devices with their start and end apart: 5 -> 2, of which waited for: 5 -> 2; matrix products, arithmetic and copies ran while one was open for 9% -> 1% of each run, Pallas kernels for 0% -> 0%
where the time goes in v1:
time: 324 us
  Pallas kernels  195 us (60%)
  waiting for transfers between devices  73.7 us (23%)
  local copies, waits for them, and re-layouts  19.6 us (6%)
  blocking collectives  14.4 us (4%)
  between operations  14.4 us (4%)
  other arithmetic  3.77 us (1%)
    pallas_call x1, Pallas kernels, attention(): pl.pallas_call(functools.partial(attn_body, steps=steps, group=group), gr...  101 us
    pallas_call x1, Pallas kernels, moe(): pl.pallas_call(moe_body, out_shape=jax.ShapeDtypeStruct((steps, nb, width...  93.7 us
    psum x1, waiting for transfers between devices, per_device(): lax.psum(jnp.dot(mixed, wo, preferred_element_type=F32).astype(BF16), 'y')  39.3 us
    psum x1, waiting for transfers between devices, per_device(): lax.psum(jnp.dot(normed, w_all, preferred_element_type=F32).astype(BF16),...  34.3 us
    psum x2, blocking collectives, shard_norm(): sq_total = lax.psum(jnp.sum(x_f32 * x_f32, axis=-1, keepdims=True), 'x')  14.4 us
  transfers between devices with their start and end apart: 2, of which 2 were waited for; matrix products, arithmetic and copies ran while one was open for 1% of the time, Pallas kernels for 0%

profile of v1, /device:TPU:0, one launch (start us, length us, event | category | flops | bytes accessed | tf_op | source)
XLA Modules:
  0.0 323.8 jit_solution(1715585278098870383)
XLA Ops:
  7.2 0.0 all-reduce.7.cloned.1.call-start
  7.2 0.7 reshape.176
  7.9 0.7 copy.46
  8.6 0.0 copy-start.4
  8.7 5.0 %gather_fusion = bf16[768,384]{1,0:T(8,128)(2,1)S(1)} fusion(bf16[49152,384]{1,0:T(8,128)(2,1)} %param.19, s32[1024]{0:T(1024)S(1)} %pad_clamp_fusion), kind=kCustom, calls=%fused_computation | custom fusion | bytes 1182720 | tf_op jit(solution)/shard_map/jit(_take)/gather | solution.py:370
  13.7 0.0 copy-start.6
  13.7 0.0 copy-start.7
  13.7 0.0 copy-start.10
  13.7 0.3 fusion.3
  14.1 8.4 %psum.28 = f32[768,1]{0,1:T(1,128)S(1)} all-reduce(f32[768,1]{0,1:T(1,128)S(1)} %broadcast_in_dim.30), channel_id=1, replica_groups=mesh['dp'=2,'y'=4,'x'=4] {'x'}, use_global_device_ids=true, to_apply=%region_1.2 | all-reduce | flops 768 | bytes 6144 | tf_op jit(solution)/shard_map/psum | solution.py:331
  22.5 0.0 copy-done.4
  22.5 0.2 copy.33
  22.8 0.0 copy-done.6
  22.8 0.1 copy.35
  22.9 0.0 copy-done.7
  23.0 0.1 copy.36
  23.1 0.0 copy-done.10
  23.1 0.0 copy-start
  23.1 1.8 convolution_convert_fusion
  24.9 0.0 all-reduce.7.cloned.1.call-update
  24.9 0.0 all-reduce.9.cloned.1.call-start
  25.0 0.0 copy-done
  25.0 0.9 copy-done.5
  25.8 0.7 copy.44
  26.6 0.4 multiply_cosine_fusion
  27.0 34.3 %all-reduce.7.cloned.1.call-done = bf16[768,640]{1,0:T(8,128)(2,1)} async-done(((bf16[768,640]{1,0:T(8,128)(2,1)}), bf16[768,640]{1,0:T(8,128)(2,1)}) %all-reduce.7.cloned.1.call-update) | async-done | bytes 983056 | tf_op jit(solution)/shard_map/psum | solution.py:372
  61.4 1.1 slice-done
  62.5 0.3 copy.37
  62.8 0.2 fusion.10
  63.1 0.1 reshape.183
  63.2 0.2 copy.40
  63.4 0.8 reshape.184
  64.3 0.3 reshape.181
  64.5 0.0 copy-start.3
  64.6 0.8 copy.38
  65.4 0.4 copy.39
  65.8 0.0 copy-done.3
  65.9 0.0 slice-start.1
  65.9 0.2 pad.15.q_ref
  66.1 0.7 slice-done.1
  66.8 0.2 copy.48
  67.0 0.2 reshape.186
  67.2 101.0 %shard_map.175 = (bf16[256,16,128]{2,1,0:T(8,128)(2,1)S(1)}, bf16[256,128,256]{2,1,0:T(8,128)(2,1)}, bf16[256,128,256]{2,1,0:T(8,128)(2,1)}) custom-call(s32[256]{0:T(256)S(1)} %copy-done, bf16[256,16,128]{2,1,0:T(8,128)(2,1)S(1)} %pad.15.q_ref, bf16[32,32,128]{2,1,0:T(8,128)(2,1)S(1)} %pad.16.kn_ref, bf16[32,32,128]{2,1,0:T(8,128)(2,1)S(1)} %pad.17.vn_ref, ...), custom_call_target="tpu_custom_call" | custom-call | flops 1073741824 | bytes 67108864 | tf_op jit(solution)/shard_map/pallas_call | solution.py:65
  168.2 0.7 copy.42
  169.0 0.3 copy.43
  169.3 0.0 copy-start.11
  169.3 0.0 copy-start.9
  169.3 0.0 copy-start.8
  169.3 0.0 copy-done.2
  169.3 1.3 convolution_convert_fusion.1
  170.6 0.0 all-reduce.9.cloned.1.call-update
  170.7 0.0 copy-done.11
  170.7 0.0 copy-done.9
  170.7 0.0 copy-done.8
  170.7 0.1 copy.45
  170.8 0.7 pad.18.wr_ref
  171.5 39.3 %all-reduce.9.cloned.1.call-done = bf16[768,384]{1,0:T(8,128)(2,1)} async-done(((bf16[768,384]{1,0:T(8,128)(2,1)}), bf16[768,384]{1,0:T(8,128)(2,1)}) %all-reduce.9.cloned.1.call-update) | async-done | bytes 589840 | tf_op jit(solution)/shard_map/psum | solution.py:386
  210.8 1.6 fusion
  212.4 0.0 copy-start.1
  212.4 6.0 %psum.31 = f32[768,1]{0,1:T(1,128)S(1)} all-reduce(f32[768,1]{0,1:T(1,128)S(1)} %broadcast_in_dim.31), channel_id=1, replica_groups=mesh['dp'=2,'y'=4,'x'=4] {'x'}, use_global_device_ids=true, to_apply=%region_5.6 | all-reduce | flops 768 | bytes 6144 | tf_op jit(solution)/shard_map/psum | solution.py:331
  218.4 1.0 fusion.2.h_ref
  219.4 1.8 broadcast_in_dim.32.chb_ref
  221.3 93.7 %shard_map.176 = bf16[3,256,384]{2,1,0:T(8,128)(2,1)} custom-call(bf16[768,384]{1,0:T(8,128)(2,1)} %fusion.2.h_ref, bf16[768,384]{1,0:T(8,128)(2,1)} %copy-done.1, bf16[384,128]{1,0:T(8,128)(2,1)} %pad.18.wr_ref, bf16[8,768,128]{2,1,0:T(8,128)(2,1)} %broadcast_in_dim.32.chb_ref, bf16[40,384,128]{2,1,0:T(8,128)(2,1)} %wact_hbm.1, ...), custom_call_target="tpu_custom_call" | custom-call | flops 9059696640 | bytes 12582912 | tf_op jit(solution)/shard_map/pallas_call | solution.py:299
  315.0 1.9 copy.52
  (22 shorter events, 0.3 us)
Async XLA Ops:
  7.2 54.2 %all-reduce.7.cloned.1.call-start = ((), (), s32[]{:S(2)}) async-start(), calls=%async_computation | async-start | bytes 1966080 | tf_op jit(solution)/shard_map/psum | solution.py:372
  8.6 13.9 %copy-start.4 = (bf16[384,384]{1,0:T(8,128)(2,1)S(1)}, bf16[384,384]{1,0:T(8,128)(2,1)}, u32[]{:S(2)}) copy-start(bf16[384,384]{1,0:T(8,128)(2,1)} %param.23) | copy-start | bytes 884740
  13.7 9.1 %copy-start.6 = (bf16[384,128]{1,0:T(8,128)(2,1)S(1)}, bf16[384,128]{1,0:T(8,128)(2,1)}, u32[]{:S(2)}) copy-start(bf16[384,128]{1,0:T(8,128)(2,1)} %param.24) | copy-start | bytes 294916
  13.7 9.3 %copy-start.7 = (bf16[384,128]{1,0:T(8,128)(2,1)S(1)}, bf16[384,128]{1,0:T(8,128)(2,1)}, u32[]{:S(2)}) copy-start(bf16[384,128]{1,0:T(8,128)(2,1)} %param.25) | copy-start | bytes 294916
  13.7 9.4 %copy-start.10 = (bf16[384]{0:T(512)(128)(2,1)S(1)}, bf16[384]{0:T(512)(128)(2,1)}, u32[]{:S(2)}) copy-start(bf16[384]{0:T(512)(128)(2,1)} %param.22) | copy-start | bytes 2308
  23.1 1.9 copy-start
  24.9 1.0 copy-start.5
  24.9 185.9 %all-reduce.9.cloned.1.call-start = ((), (), s32[]{:S(2)}) async-start(), calls=%async_computation.1 | async-start | bytes 1179648 | tf_op jit(solution)/shard_map/psum | solution.py:386
  61.4 1.1 slice-start
  64.5 1.3 copy-start.3
  65.9 0.9 slice-start.1
  168.2 1.1 copy-start.2
  169.3 1.4 copy-start.11
  169.3 1.4 copy-start.9
  169.3 1.4 copy-start.8
  212.4 8.9 %copy-start.1 = (bf16[768,384]{1,0:T(8,128)(2,1)}, bf16[768,384]{1,0:T(8,128)(2,1)S(1)}, u32[]{:S(2)}) copy-start(bf16[768,384]{1,0:T(8,128)(2,1)S(1)} %get-tuple-element.10.xm_ref) | copy-start | bytes 1769476
Sparse Core Ops, SparseCore 0:
  25.0 36.3 all-reduce.6
  170.8 39.9 all-reduce.8

commit v2 on v1

v2 whole, which is shorter than its diff:
```python
import functools
import jax
import jax.numpy as jnp
from jax import lax
from jax.experimental import pallas as pl
from jax.experimental.pallas import tpu as pltpu
from jax.sharding import PartitionSpec as P

EPS = 1e-5
ROPE_BASE = 1.0e6
MESH = pl.DeviceIdType.MESH
F32 = jnp.float32
BF16 = jnp.bfloat16
LANE = 128
SUB = 16
MIB = 1024 * 1024
LOWEST = -1.0e30
NB = 16
QROWS = 16


def attn_body(len_ref, q_ref, kn_ref, vn_ref, k_ref, v_ref, o_ref, ko_ref, vo_ref, s_ref, w_ref, *, steps, group):
    half, seq = k_ref.shape[1:]
    n_seq = k_ref.shape[0]
    step = pl.program_id(0)
    fill = jnp.zeros((LANE - kn_ref.shape[1], LANE), F32)
    kn_t = jnp.concatenate([kn_ref[0].astype(F32), fill], axis=0).T
    vn_t = jnp.concatenate([vn_ref[0].astype(F32), fill], axis=0).T
    lane = lax.broadcasted_iota(jnp.int32, (SUB, LANE), 1).astype(F32).astype(BF16)
    srow = lax.broadcasted_iota(jnp.int32, (2 * QROWS, seq), 0)
    scol = lax.broadcasted_iota(jnp.int32, (2 * QROWS, seq), 1)
    srow = jnp.where(srow >= QROWS, srow - QROWS, srow)
    rel = scol - jnp.where(srow >= 2 * group, 2, jnp.where(srow >= group, 1, 0))
    low = lax.broadcasted_iota(jnp.int32, (QROWS, LANE), 1) < 64
    low_b = lane < jnp.asarray(64, BF16)
    for b in range(n_seq):
        pos = len_ref[step * n_seq + b]
        turn = lax.rem(pos + LANE - b * steps, LANE)
        new = (pltpu.roll(kn_t, turn, 1).astype(BF16), pltpu.roll(vn_t, turn, 1).astype(BF16))
        gap = lane - jnp.full((SUB, LANE), pos.astype(F32), F32).astype(BF16)
        for tile in range(seq // LANE):
            lo = jnp.asarray(-LANE * tile, BF16)
            hi = jnp.asarray(steps - 1 - LANE * tile, BF16)
            hit = (gap >= lo) & (gap <= hi)
            for i in range(half // SUB):
                rs, cs = slice(SUB * i, SUB * i + SUB), slice(LANE * tile, LANE * tile + LANE)
                ko_ref[b, rs, cs] = jnp.where(hit, new[0][rs], k_ref[b, rs, cs])
                vo_ref[b, rs, cs] = jnp.where(hit, new[1][rs], v_ref[b, rs, cs])
    for b in range(n_seq):
        q16 = q_ref[b]
        zero = jnp.zeros_like(q16)
        q32 = jnp.concatenate([jnp.where(low_b, q16, zero), jnp.where(low_b, zero, q16)], axis=0)
        s_ref[b] = jnp.dot(q32, ko_ref[b], preferred_element_type=F32)
    tots = []
    for b in range(n_seq):
        pos = len_ref[step * n_seq + b]
        ok = rel <= pos
        s = jnp.where(ok, s_ref[b] * 0.125, LOWEST)
        peak = jnp.max(s, axis=1, keepdims=True)
        w = jnp.where(ok, jnp.exp(s - peak), 0.0)
        tots.append(jnp.sum(w, axis=1, keepdims=True))
        w_ref[b] = w.astype(BF16)
    for b in range(n_seq):
        o = lax.dot_general(w_ref[b], vo_ref[b], (((1,), (1,)), ((), ())), preferred_element_type=F32)
        o = o / tots[b]
        o_ref[b] = jnp.where(low, o[:QROWS], o[QROWS:]).astype(BF16)


def attention(lengths, q, kn, vn, kc, vc, steps, group):
    nb, half, seq = kc.shape
    grid = nb // NB
    cache = pl.BlockSpec((NB, half, seq), lambda i, l: (i, 0, 0))
    new = pl.BlockSpec((1,) + kn.shape[1:], lambda i, l: (i, 0, 0))
    qs = pl.BlockSpec((NB, QROWS, LANE), lambda i, l: (i, 0, 0))
    return pl.pallas_call(
        functools.partial(attn_body, steps=steps, group=group),
        grid_spec=pltpu.PrefetchScalarGridSpec(num_scalar_prefetch=1, grid=(grid,), in_specs=[qs, new, new, cache, cache], out_specs=[qs, cache, cache], scratch_shapes=[pltpu.VMEM((NB, 2 * QROWS, seq), F32), pltpu.VMEM((NB, 2 * QROWS, seq), BF16)]),
        out_shape=[jax.ShapeDtypeStruct((nb, QROWS, LANE), BF16), jax.ShapeDtypeStruct(kc.shape, BF16), jax.ShapeDtypeStruct(vc.shape, BF16)],
        compiler_params=pltpu.CompilerParams(vmem_limit_bytes=40 * MIB, dimension_semantics=("arbitrary",)),
        cost_estimate=pl.CostEstimate(flops=2 * nb * 32 * LANE * seq * 2, bytes_accessed=4 * nb * half * seq * 2, transcendentals=0),
    )(lengths, q, kn, vn, kc, vc)


def remote(src, dst, ssem, rsem, dev):
    return pltpu.make_async_remote_copy(src_ref=src, dst_ref=dst, send_sem=ssem, recv_sem=rsem, device_id=dev, device_id_type=MESH)


def square_rows(x_f32):
    tiles = x_f32.shape[1] // LANE
    acc = x_f32[:, 0:LANE] * x_f32[:, 0:LANE]
    for i in range(1, tiles):
        part = x_f32[:, LANE * i:LANE * (i + 1)]
        acc = acc + part * part
    return jnp.sum(acc.T, axis=0, keepdims=True)


def scale_rows(x_f32, stat_row, gain, width_full):
    scale = lax.rsqrt(stat_row / width_full + EPS)
    col = jnp.broadcast_to(scale, (LANE, LANE)).T
    parts = [x_f32[:, LANE * i:LANE * (i + 1)] * col * gain[:, LANE * i:LANE * (i + 1)] for i in range(x_f32.shape[1] // LANE)]
    return jnp.concatenate(parts, axis=1).astype(BF16)


def front_body(x_ref, g_ref, w_ref, cos_ref, sin_ref, out_ref, st, st_in, hh, pj, rs1, cs, rs2, sts, str_, s1s, s1r, s2s, s2r, s3s, s3r, *, width_full, turn_cols):
    steps, nb = out_ref.shape[:2]
    cols = out_ref.shape[2]
    hb = nb // 2
    dp, y, x = lax.axis_index("dp"), lax.axis_index("y"), lax.axis_index("x")
    core, chip = x % 2, x // 2
    sib = (dp, y, chip * 2 + (1 - core))
    peer = (dp, y, (1 - chip) * 2 + core)
    diag = (dp, y, (1 - chip) * 2 + (1 - core))
    near = (sib, peer, diag)
    barrier = pltpu.get_barrier_semaphore()
    for dev in near:
        pl.semaphore_signal(barrier, inc=1, device_id=dev, device_id_type=MESH)
    keep = pl.multiple_of(core * hb, hb)
    give = pl.multiple_of((1 - core) * hb, hb)
    st[...] = jnp.zeros_like(st)
    blocks = steps * nb // LANE
    for i in range(blocks):
        st[i:i + 1, :] = square_rows(x_ref[LANE * i:LANE * (i + 1), :].astype(F32))
    pl.semaphore_wait(barrier, 3)
    stat = [remote(st, st_in.at[k], sts.at[k], str_.at[k], near[k]) for k in range(3)]
    for k in range(3):
        stat[k].start()
    for k in range(3):
        stat[k].wait_recv()
    total = st[...] + st_in[0] + st_in[1] + st_in[2]

    def s1(c):
        return remote(pj.at[c, pl.ds(give, hb), :], rs1.at[c], s1s.at[c], s1r.at[c], sib)

    def s2(c):
        return remote(cs.at[c], rs2.at[c], s2s.at[c], s2r.at[c], peer)

    def s3(c, row):
        return remote(out_ref.at[c, pl.ds(row, hb), :], out_ref.at[c, pl.ds(row, hb), :], s3s.at[c], s3r.at[c], sib)

    def mid(c):
        s1(c).wait_recv()
        cs[c] = (pj[c, pl.ds(keep, hb), :].astype(F32) + rs1[c].astype(F32)).astype(BF16)
        s2(c).start()

    def last(c):
        s2(c).wait_recv()
        fin = (cs[c].astype(F32) + rs2[c].astype(F32)).astype(BF16).astype(F32)
        cosv = cos_ref[c, pl.ds(keep, hb), :]
        sinv = sin_ref[c, pl.ds(keep, hb), :]
        first = lax.broadcasted_iota(jnp.int32, (hb, LANE), 1) % 64 < 32
        for i in range(cols // LANE):
            v = fin[:, LANE * i:LANE * (i + 1)]
            if i < turn_cols // LANE:
                swap = jnp.where(first, pltpu.roll(v, 96, 1), pltpu.roll(v, 32, 1))
                v = v * cosv + swap * sinv
            out_ref[c, pl.ds(keep, hb), LANE * i:LANE * (i + 1)] = v.astype(BF16)
        s3(c, keep).start()

    for c in range(steps):
        for i in range(c * nb // LANE, (c + 1) * nb // LANE):
            hh[LANE * i:LANE * (i + 1), :] = scale_rows(x_ref[LANE * i:LANE * (i + 1), :].astype(F32), total[i:i + 1, :], g_ref[...], width_full)
        pj[c] = jnp.dot(hh[c * nb:(c + 1) * nb, :], w_ref[...], preferred_element_type=F32).astype(BF16)
        s1(c).start()
        if c >= 1:
            mid(c - 1)
    mid(steps - 1)
    for c in range(steps):
        last(c)
    for c in range(steps):
        s3(c, give).wait_recv()
    for k in range(3):
        stat[k].wait_send()
    for c in range(steps):
        s1(c).wait_send()
        s2(c).wait_send()
        s3(c, keep).wait_send()


def front(x_in, gain, w_all, cosv, sinv, steps, width_full, turn_cols):
    rows, width = x_in.shape
    nb = rows // steps
    cols = w_all.shape[1]
    hb = nb // 2
    dma = pltpu.SemaphoreType.DMA
    vm = pl.BlockSpec(memory_space=pltpu.VMEM)
    return pl.pallas_call(
        functools.partial(front_body, width_full=width_full, turn_cols=turn_cols),
        out_shape=jax.ShapeDtypeStruct((steps, nb, cols), BF16),
        in_specs=[vm] * 5,
        out_specs=vm,
        scratch_shapes=[
            pltpu.VMEM((8, LANE), F32), pltpu.VMEM((3, 8, LANE), F32),
            pltpu.VMEM((rows, width), BF16), pltpu.VMEM((steps, nb, cols), BF16),
            pltpu.VMEM((steps, hb, cols), BF16), pltpu.VMEM((steps, hb, cols), BF16), pltpu.VMEM((steps, hb, cols), BF16),
            dma((3,)), dma((3,)), dma((steps,)), dma((steps,)), dma((steps,)), dma((steps,)), dma((steps,)), dma((steps,)),
        ],
        compiler_params=pltpu.CompilerParams(collective_id=2, has_side_effects=True, vmem_limit_bytes=24 * MIB),
        cost_estimate=pl.CostEstimate(flops=2 * rows * width * cols, bytes_accessed=4 * MIB, transcendentals=0),
    )(x_in, gain, w_all, cosv, sinv)


def tail_body(mix_ref, wo_ref, xin_ref, g_ref, wr_ref, chb_ref, wact_hbm, wlin_hbm, wdn_hbm, out_ref,
              wcat, wdn, pa, ar, xm, hh, st, st_in, hs, rs1, cs, rs2, lgp, lr1, lcs, lr2, u, pd, yr,
              wsem, as_, ar_s, xs, xr, sts, str_, s1s, s1r, s2s, s2r, l1s, l1r, l2s, l2r, us, ur, ys, yrs, gs, gr, *, width_full):
    experts = wcat.shape[0]
    ff = wact_hbm.shape[2]
    steps, nb = hs.shape[:2]
    hb, qb = nb // 2, nb // 4
    top = chb_ref.shape[0]
    dp, y, x = lax.axis_index("dp"), lax.axis_index("y"), lax.axis_index("x")
    core, chip = x % 2, x // 2
    sib = (dp, y, chip * 2 + (1 - core))
    peer = (dp, y, (1 - chip) * 2 + core)
    diag = (dp, y, (1 - chip) * 2 + (1 - core))
    near = (sib, peer, diag)
    ypeer = [None] + [(dp, (y + d) % 4, x) for d in (1, 2, 3)]

    w0 = pltpu.make_async_copy(wact_hbm, wcat.at[:, :, pl.ds(0, ff)], wsem.at[0])
    w1 = pltpu.make_async_copy(wlin_hbm, wcat.at[:, :, pl.ds(ff, ff)], wsem.at[1])
    w2 = pltpu.make_async_copy(wdn_hbm, wdn, wsem.at[2])
    barrier = pltpu.get_barrier_semaphore()
    for dev in near + tuple(ypeer[1:]):
        pl.semaphore_signal(barrier, inc=1, device_id=dev, device_id_type=MESH)

    keep = pl.multiple_of(core * hb, hb)
    give = pl.multiple_of((1 - core) * hb, hb)
    sub_keep = pl.multiple_of(chip * qb, qb)
    sub_give = pl.multiple_of((1 - chip) * qb, qb)
    own = pl.multiple_of(core * hb + chip * qb, qb)
    other = pl.multiple_of(core * hb + (1 - chip) * qb, qb)
    sib_own = pl.multiple_of((1 - core) * hb + chip * qb, qb)
    sib_other = pl.multiple_of((1 - core) * hb + (1 - chip) * qb, qb)
    yrow = pl.multiple_of(y * qb, qb)

    def yblock(k):
        return pl.multiple_of(((y + k) % 4) * qb, qb)

    def rs_send(buf, land, ssem, rsem, c, d):
        return remote(buf.at[c, pl.ds(yblock(d), qb), :], land.at[c, 3 - d], ssem.at[c, d - 1], rsem.at[c, 3 - d], ypeer[d])

    def rs_recv(buf, land, ssem, rsem, c, k):
        return remote(buf.at[c, pl.ds(0, qb), :], land.at[c, k], ssem.at[c, k], rsem.at[c, k], ypeer[1])

    def ag_send(buf, ssem, rsem, c, d):
        return remote(buf.at[c, pl.ds(yrow, qb), :], buf.at[c, pl.ds(yrow, qb), :], ssem.at[c, d - 1], rsem.at[c, 3 - d], ypeer[d])

    def ag_recv(buf, ssem, rsem, c, k):
        row = yblock(k + 1)
        return remote(buf.at[c, pl.ds(row, qb), :], buf.at[c, pl.ds(row, qb), :], ssem.at[c, k], rsem.at[c, k], ypeer[1])

    def s1(c):
        return remote(hs.at[c, pl.ds(give, hb), :], rs1.at[c], s1s.at[c], s1r.at[c], sib)

    def s2(c):
        return remote(cs.at[c], rs2.at[c], s2s.at[c], s2r.at[c], peer)

    def l1(c):
        return remote(lgp.at[c, pl.ds(give, hb), :], lr1.at[c], l1s.at[c], l1r.at[c], sib)

    def l2(c):
        return remote(lcs.at[c], lr2.at[c], l2s.at[c], l2r.at[c], peer)

    def u_peer(c, row):
        return remote(u.at[c, pl.ds(row, qb), :], u.at[c, pl.ds(row, qb), :], us.at[c, 0], ur.at[c, 0], peer)

    def u_sib(c, row, k):
        return remote(u.at[c, pl.ds(row, qb), :], u.at[c, pl.ds(row, qb), :], us.at[c, k], ur.at[c, k], sib)

    def stat(c, k):
        return remote(st.at[c], st_in.at[c, k], sts.at[c, k], str_.at[c, k], near[k])

    def attn_out(c):
        pa[c] = jnp.dot(mix_ref[c * nb:(c + 1) * nb, :], wo_ref[...], preferred_element_type=F32).astype(BF16)

    def attn_send(c):
        for d in (1, 2, 3):
            rs_send(pa, ar, as_, ar_s, c, d).start()

    def attn_sum(c):
        for k in range(3):
            rs_recv(pa, ar, as_, ar_s, c, k).wait_recv()
        acc = pa[c, pl.ds(yrow, qb), :].astype(F32)
        for k in range(3):
            acc = acc + ar[c, k].astype(F32)
        base = xin_ref[pl.ds(pl.multiple_of(c * nb + yrow, qb), qb), :].astype(F32)
        xm[c, pl.ds(yrow, qb), :] = (base + acc).astype(BF16)
        for d in (1, 2, 3):
            ag_send(xm, xs, xr, c, d).start()

    def stats(c):
        for k in range(3):
            ag_recv(xm, xs, xr, c, k).wait_recv()
        for i in range(nb // LANE):
            st[c, i:i + 1, :] = square_rows(xm[c, LANE * i:LANE * (i + 1), :].astype(F32))
        for k in range(3):
            stat(c, k).start()

    def norm(c):
        for k in range(3):
            stat(c, k).wait_recv()
        total = st[c] + st_in[c, 0] + st_in[c, 1] + st_in[c, 2]
        for i in range(nb // LANE):
            hh[c, LANE * i:LANE * (i + 1), :] = scale_rows(xm[c, LANE * i:LANE * (i + 1), :].astype(F32), total[i:i + 1, :], g_ref[...], width_full)
        lgp[c] = jnp.dot(hh[c], wr_ref[...], preferred_element_type=F32)
        l1(c).start()

    def experts_in(c, hd):
        span = 4

        def few(i, carry):
            for k in range(span):
                e = i * span + k
                hval = jnp.dot(hh[c], wcat[e], preferred_element_type=F32)
                hd[e, :, 0:ff] = hval[:, 0:ff].astype(BF16)
                hd[experts + e, :, 0:ff] = hval[:, ff:2 * ff].astype(BF16)
            return carry
        lax.fori_loop(0, experts // span, few, 0)

    def pick(c, hd, chs):
        def tile(i, carry):
            r = pl.multiple_of(i * SUB, SUB)
            ch = [chs[j, pl.ds(pl.multiple_of(c * nb + i * SUB, SUB), SUB), :] for j in range(top)]
            span = 8

            def some(g, state):
                acc, ev = list(state[0]), state[1]
                for k in range(span):
                    e = g * span + k
                    va = hd[e, pl.ds(r, SUB), :]
                    vl = hd[experts + e, pl.ds(r, SUB), :]
                    for j in range(top):
                        m = ch[j] == ev
                        acc[2 * j] = jnp.where(m, va, acc[2 * j])
                        acc[2 * j + 1] = jnp.where(m, vl, acc[2 * j + 1])
                    ev = ev + jnp.ones_like(ev)
                return tuple(acc), ev
            zero = jnp.zeros((SUB, ff), BF16)
            acc, _ = lax.fori_loop(0, experts // span, some, (tuple(zero for _ in range(2 * top)), zero))
            for k in range(2 * top):
                hs[c, pl.ds(r, SUB), k * ff:(k + 1) * ff] = acc[k]
            return carry
        lax.fori_loop(0, nb // SUB, tile, 0)

    def logits_mid(c):
        l1(c).wait_recv()
        lcs[c] = lgp[c, pl.ds(other, qb), :] + lr1[c, pl.ds(sub_give, qb), :]
        l2(c).start()

    def part_b(c):
        s1(c).wait_recv()

        def add(i, carry):
            r = pl.multiple_of(i * SUB, SUB)
            mine = hs[c, pl.ds(pl.multiple_of(other + r, SUB), SUB), :].astype(F32)
            got = rs1[c, pl.ds(pl.multiple_of(sub_give + r, SUB), SUB), :].astype(F32)
            cs[c, pl.ds(r, SUB), :] = (mine + got).astype(BF16)
            return carry
        lax.fori_loop(0, qb // SUB, add, 0)
        s2(c).start()

    def part_u(c):
        l2(c).wait_recv()
        s2(c).wait_recv()

        def tile(i, carry):
            r = pl.multiple_of(i * SUB, SUB)
            r_own = pl.multiple_of(own + r, SUB)
            r_sub = pl.multiple_of(sub_keep + r, SUB)
            logit = lgp[c, pl.ds(r_own, SUB), :] + lr1[c, pl.ds(r_sub, SUB), :] + lr2[c, pl.ds(r, SUB), :]
            lane = lax.broadcasted_iota(jnp.int32, (SUB, LANE), 1).astype(F32)
            hit = [chb_ref[j, pl.ds(pl.multiple_of(c * nb + own + r, SUB), SUB), :].astype(F32) == lane for j in range(top)]
            any_hit = hit[0]
            for j in range(1, top):
                any_hit = any_hit | hit[j]
            peak = jnp.max(jnp.where(any_hit, logit, -jnp.inf), axis=1, keepdims=True)
            ex = jnp.where(any_hit, jnp.exp(logit - peak), 0.0)
            coef = ex / jnp.sum(ex, axis=1, keepdims=True)
            for j in range(top):
                gate = jnp.sum(jnp.where(hit[j], coef, 0.0), axis=1, keepdims=True)
                ca, cl = pl.ds(2 * j * ff, ff), pl.ds((2 * j + 1) * ff, ff)
                act = hs[c, pl.ds(r_own, SUB), ca].astype(F32) + rs1[c, pl.ds(r_sub, SUB), ca].astype(F32) + rs2[c, pl.ds(r, SUB), ca].astype(F32)
                lin = hs[c, pl.ds(r_own, SUB), cl].astype(F32) + rs1[c, pl.ds(r_sub, SUB), cl].astype(F32) + rs2[c, pl.ds(r, SUB), cl].astype(F32)
                val = gate * (act / (1.0 + jnp.exp(-act))) * lin
                u[c, pl.ds(r_own, SUB), j * ff:(j + 1) * ff] = val.astype(BF16)
            return carry
        lax.fori_loop(0, qb // SUB, tile, 0)
        u_peer(c, own).start()
        u_sib(c, own, 1).start()

    def part_f(c):
        u_peer(c, other).wait_recv()
        u_sib(c, other, 2).start()

    def part_d(c, ud, chs, us16):
        u_sib(c, sib_own, 1).wait_recv()
        u_sib(c, sib_other, 2).wait_recv()
        for j in range(top):
            us16[j] = u[c, :, j * ff:(j + 1) * ff]

        def spread(i, carry):
            r = pl.multiple_of(i * SUB, SUB)
            ch = [chs[j, pl.ds(pl.multiple_of(c * nb + i * SUB, SUB), SUB), :] for j in range(top)]
            vals = [us16[j, pl.ds(r, SUB), :] for j in range(top)]
            for e in range(experts):
                acc = jnp.zeros((SUB, ff), BF16)
                for j in range(top):
                    acc = jnp.where(ch[j] == jnp.asarray(e, BF16), vals[j], acc)
                ud[pl.ds(r, SUB), e * ff:(e + 1) * ff] = acc
            return carry
        lax.fori_loop(0, nb // SUB, spread, 0)
        pd[c] = jnp.dot(ud[...], wdn[...], preferred_element_type=F32).astype(BF16)
        for d in (1, 2, 3):
            rs_send(pd, yr, ys, yrs, c, d).start()

    def part_g(c):
        for k in range(3):
            rs_recv(pd, yr, ys, yrs, c, k).wait_recv()
        acc = pd[c, pl.ds(yrow, qb), :].astype(F32)
        for k in range(3):
            acc = acc + yr[c, k].astype(F32)
        out_ref[c, pl.ds(yrow, qb), :] = (xm[c, pl.ds(yrow, qb), :].astype(F32) + acc).astype(BF16)
        for d in (1, 2, 3):
            ag_send(out_ref, gs, gr, c, d).start()

    def run(hd, ud, chs, us16):
        attn_out(0)
        pl.semaphore_wait(barrier, 6)
        attn_send(0)
        attn_out(1)
        attn_send(1)
        w0.start()
        w1.start()
        w2.start()
        st[...] = jnp.zeros_like(st)
        for j in range(top):
            chs[j] = chb_ref[j]
        attn_out(2)
        attn_sum(0)
        attn_send(2)
        attn_sum(1)
        attn_sum(2)
        stats(0)
        norm(0)
        w0.wait()
        w1.wait()
        experts_in(0, hd)
        logits_mid(0)
        stats(1)
        pick(0, hd, chs)
        s1(0).start()
        norm(1)
        stats(2)
        experts_in(1, hd)
        part_b(0)
        logits_mid(1)
        norm(2)
        pick(1, hd, chs)
        s1(1).start()
        experts_in(2, hd)
        part_u(0)
        part_b(1)
        logits_mid(2)
        pick(2, hd, chs)
        s1(2).start()
        part_f(0)
        part_u(1)
        part_b(2)
        w2.wait()
        part_d(0, ud, chs, us16)
        part_f(1)
        part_u(2)
        part_d(1, ud, chs, us16)
        part_f(2)
        part_g(0)
        part_d(2, ud, chs, us16)
        part_g(1)
        part_g(2)

    bf = functools.partial(pltpu.VMEM, dtype=BF16)
    pl.run_scoped(run, bf((2 * experts, nb, ff)), bf((nb, experts * ff)), bf((top, steps * nb, ff)), bf((top, nb, ff)))

    for c in range(steps):
        for k in range(3):
            ag_recv(out_ref, gs, gr, c, k).wait_recv()
    for c in range(steps):
        l1(c).wait_send()
        l2(c).wait_send()
        s1(c).wait_send()
        s2(c).wait_send()
        u_peer(c, own).wait_send()
        u_sib(c, own, 1).wait_send()
        u_sib(c, other, 2).wait_send()
        for k in range(3):
            stat(c, k).wait_send()
        for d in (1, 2, 3):
            rs_send(pa, ar, as_, ar_s, c, d).wait_send()
            ag_send(xm, xs, xr, c, d).wait_send()
            rs_send(pd, yr, ys, yrs, c, d).wait_send()
            ag_send(out_ref, gs, gr, c, d).wait_send()


def tail(mixed, wo, x_in, gain, w_router, chb, w_act, w_lin, w_down, steps, width_full):
    rows, width = x_in.shape
    nb = rows // steps
    experts, _, ff = w_act.shape
    top = chb.shape[0]
    hb, qb = nb // 2, nb // 4
    dma = pltpu.SemaphoreType.DMA
    vm = pl.BlockSpec(memory_space=pltpu.VMEM)
    hbm = pl.BlockSpec(memory_space=pl.ANY)
    sems = [(steps, 3)] * 6 + [(steps,)] * 8 + [(steps, 3)] * 6
    return pl.pallas_call(
        functools.partial(tail_body, width_full=width_full),
        out_shape=jax.ShapeDtypeStruct((steps, nb, width), BF16),
        in_specs=[vm] * 6 + [hbm] * 3,
        out_specs=vm,
        scratch_shapes=[
            pltpu.VMEM((experts, width, 2 * ff), BF16),
            pltpu.VMEM((experts * ff, width), BF16),
            pltpu.VMEM((steps, nb, width), BF16),
            pltpu.VMEM((steps, 3, qb, width), BF16),
            pltpu.VMEM((steps, nb, width), BF16),
            pltpu.VMEM((steps, nb, width), BF16),
            pltpu.VMEM((steps, 8, LANE), F32),
            pltpu.VMEM((steps, 3, 8, LANE), F32),
            pltpu.VMEM((steps, nb, 2 * top * ff), BF16),
            pltpu.VMEM((steps, hb, 2 * top * ff), BF16),
            pltpu.VMEM((steps, qb, 2 * top * ff), BF16),
            pltpu.VMEM((steps, qb, 2 * top * ff), BF16),
            pltpu.VMEM((steps, nb, LANE), F32),
            pltpu.VMEM((steps, hb, LANE), F32),
            pltpu.VMEM((steps, qb, LANE), F32),
            pltpu.VMEM((steps, qb, LANE), F32),
            pltpu.VMEM((steps, nb, top * ff), BF16),
            pltpu.VMEM((steps, nb, width), BF16),
            pltpu.VMEM((steps, 3, qb, width), BF16),
            dma((3,)),
        ] + [dma(n) for n in sems],
        compiler_params=pltpu.CompilerParams(collective_id=1, has_side_effects=True, vmem_limit_bytes=60 * MIB),
        cost_estimate=pl.CostEstimate(flops=6 * rows * width * experts * ff, bytes_accessed=12 * MIB, transcendentals=0),
    )(mixed, wo, x_in, gain, w_router, chb, w_act, w_lin, w_down.reshape(experts * ff, width))


def turn_tables(positions, head_dim):
    half_dim = head_dim // 2
    inv_freq = ROPE_BASE ** (-(jnp.arange(half_dim, dtype=F32) * 2.0 / head_dim))
    angles = positions.astype(F32)[:, None] * inv_freq[None, :]
    cosine, sine_val = jnp.cos(angles), jnp.sin(angles)
    return jnp.tile(cosine, (1, 4)), jnp.tile(jnp.concatenate([-sine_val, sine_val], axis=1), (1, 2))


def solution(mesh):
    x_count = mesh.shape['x']
    cache_spec = P('dp', None, 'y', None)
    in_specs = (P(None, 'dp'), P('dp'), P(None, 'dp', None), P(None, 'x'), cache_spec, cache_spec, P('x'), P('x', 'y'), P('x', 'y'), P('x', 'y'), P('y', 'x'), P('x'), P('x', None), P(None, 'x', 'y'), P(None, 'x', 'y'), P(None, 'y', 'x'))
    out_specs = (P(None, 'dp', 'x'), cache_spec, cache_spec)

    def per_device(tokens, lengths, choices, emb_table, k_cache, v_cache, g_attn, w_q, w_k, w_v, w_o, g_ffn, w_router, w_act, w_lin, w_down):
        steps, nb = tokens.shape
        seq, kvl, hdim = k_cache.shape[1:]
        q_cols, kv_cols = w_q.shape[1], w_k.shape[1]
        width = emb_table.shape[1]
        width_full = width * x_count
        group = q_cols // kv_cols
        rows = steps * nb
        top = choices.shape[2]
        positions = (lengths[None, :] + jnp.arange(steps, dtype=lengths.dtype)[:, None]).reshape(rows)
        wq = w_q.reshape(width, kvl, group, hdim).transpose(0, 2, 1, 3).reshape(width, q_cols)
        wo = w_o.reshape(kvl, group, hdim, width).transpose(1, 0, 2, 3).reshape(q_cols, width)
        w_all = jnp.concatenate([wq, w_k, w_v], axis=1)
        chb = jnp.broadcast_to(choices.reshape(rows, top).T.astype(BF16)[:, :, None], (top, rows, LANE))
        wr = jnp.pad(w_router, ((0, 0), (0, LANE - w_router.shape[1])))

        cosv, sinv = turn_tables(positions, hdim)
        x_in = jnp.take(emb_table, tokens.reshape(rows), axis=0)
        gain_a, gain_f = g_attn.astype(F32).reshape(1, width), g_ffn.astype(F32).reshape(1, width)
        proj = front(x_in, gain_a, w_all, cosv.reshape(steps, nb, LANE), sinv.reshape(steps, nb, LANE), steps, width_full, q_cols + kv_cols)
        q = proj[:, :, :q_cols].reshape(steps, nb, group, kv_cols).transpose(1, 0, 2, 3).reshape(nb, steps * group, kv_cols)
        q = jnp.pad(q, ((0, 0), (0, QROWS - steps * group), (0, 0)))
        kn = proj[:, :, q_cols:q_cols + kv_cols].transpose(1, 0, 2).reshape(nb // NB, NB * steps, kv_cols)
        vn = proj[:, :, q_cols + kv_cols:].transpose(1, 0, 2).reshape(nb // NB, NB * steps, kv_cols)
        pad = -(NB * steps) % 32
        kn = jnp.pad(kn, ((0, 0), (0, pad), (0, 0)))
        vn = jnp.pad(vn, ((0, 0), (0, pad), (0, 0)))
        kc = k_cache.transpose(0, 2, 3, 1).reshape(nb, kv_cols, seq)
        vc = v_cache.transpose(0, 2, 3, 1).reshape(nb, kv_cols, seq)
        o, ko, vo = attention(lengths, q, kn, vn, kc, vc, steps, group)
        mixed = o[:, :steps * group].reshape(nb, steps, q_cols).transpose(1, 0, 2).reshape(rows, q_cols)
        hidden = tail(mixed, wo, x_in, gain_f, wr, chb, w_act, w_lin, w_down, steps, width_full)
        ko = ko.reshape(nb, kvl, hdim, seq).transpose(0, 3, 1, 2)
        vo = vo.reshape(nb, kvl, hdim, seq).transpose(0, 3, 1, 2)
        return hidden, ko, vo

    return jax.shard_map(per_device, mesh=mesh, in_specs=in_specs, out_specs=out_specs, check_vma=False)
```

time: 324 us -> 178 us (0.55)
  waiting for transfers between devices: 73.7 us -> 0 us
  Pallas kernels: 195 us -> 154 us
  blocking collectives: 14.4 us -> 0 us
  between operations: 14.4 us -> 0.89 us
    psum x2 -> x0, waiting for transfers between devices: 73.6 us -> none  [the longest x1 39.3 us: per_device(): lax.psum(jnp.dot(mixed, wo, preferred_element_type=F32).astype(BF16), 'y')]
    pallas_call x1, Pallas kernels: 101 us -> 32.8 us  [attention(): pl.pallas_call(functools.partial(attn_body, steps=steps, group=group), gr...]
    pallas_call x1 -> x2, Pallas kernels: 93.7 us -> 122 us  [the longest x1 100 us: tail(): pl.pallas_call(functools.partial(tail_body, width_full=width_full), out_s...]
    psum x2 -> x0, blocking collectives: 14.4 us -> none  [shard_norm(): sq_total = lax.psum(jnp.sum(x_f32 * x_f32, axis=-1, keepdims=True), 'x')]
  transfers between devices with their start and end apart: 2 -> 0, of which waited for: 2 -> 0; matrix products, arithmetic and copies ran while one was open for 1% -> 0% of each run, Pallas kernels for 0% -> 0%
where the time goes in v2:
time: 178 us; the launch traced here: 177 us
  Pallas kernels  154 us (87%)
  local copies, waits for them, and re-layouts  19.6 us (11%)
  other arithmetic  2.42 us (1%)
    pallas_call x1, Pallas kernels, tail(): pl.pallas_call(functools.partial(tail_body, width_full=width_full), out_s...  100 us
    pallas_call x1, Pallas kernels, attention(): pl.pallas_call(functools.partial(attn_body, steps=steps, group=group), gr...  32.8 us
    pallas_call x1, Pallas kernels, front(): pl.pallas_call(functools.partial(front_body, width_full=width_full, turn_...  21.3 us
    gather x1, local copies, waits for them, and re-layouts, per_device(): x_in = jnp.take(emb_table, tokens.reshape(rows), axis=0)  5.01 us
    unnamed x16, local copies, waits for them, and re-layouts  4.18 us

profile of v2, /device:TPU:0, one launch (start us, length us, event | category | flops | bytes accessed | tf_op | source)
XLA Modules:
  0.0 177.3 jit_solution(1166508101098961949)
XLA Ops:
  0.6 0.0 copy-start.1
  0.6 0.7 add_convert_fusion
  1.4 0.4 fusion
  1.9 0.2 tile.19
  2.1 0.2 copy.30.sin_ref
  2.4 0.2 tile.17
  2.6 0.2 copy.29.cos_ref
  2.8 0.7 copy.42
  3.5 5.0 %gather_fusion = bf16[768,384]{1,0:T(8,128)(2,1)S(1)} fusion(bf16[49152,384]{1,0:T(8,128)(2,1)} %param.19, s32[1024]{0:T(1024)S(1)} %pad_clamp_fusion), kind=kCustom, calls=%fused_computation | custom fusion | bytes 1182720 | tf_op jit(solution)/shard_map/jit(_take)/gather | solution.py:575
  8.5 0.7 reshape.159
  9.2 0.2 broadcast_select_fusion.x_ref.xin_ref
  9.4 0.0 copy-start
  9.4 1.4 copy.26
  10.8 0.2 copy.28
  11.1 1.0 pad_maximum_fusion.w_ref
  12.1 0.7 reshape.181.g_ref
  12.8 21.3 %shard_map.175 = bf16[3,256,640]{2,1,0:T(8,128)(2,1)S(1)} custom-call(bf16[768,384]{1,0:T(8,128)(2,1)S(1)} %broadcast_select_fusion.x_ref.xin_ref, f32[1,384]{1,0:T(1,128)S(1)} %reshape.181.g_ref, bf16[384,640]{1,0:T(8,128)(2,1)S(1)} %pad_maximum_fusion.w_ref, f32[3,256,128]{2,1,0:T(8,128)S(1)} %copy.29.cos_ref, f32[3,256,128]{2,1,0:T(8,128)S(1)} %copy.30.sin_ref), custom_call_target="tpu_custom_call" | custom-call | flops 377487360 | bytes 4194304 | tf_op jit(solution)/shard_map/pallas_call | solution.py:186
  34.1 0.1 slice_bitcast_fusion
  34.1 0.2 copy.34
  34.3 0.2 reshape.167
  34.5 0.2 copy.35
  34.7 0.2 reshape.168
  34.9 0.1 slice.12
  34.9 0.3 copy.31
  35.2 1.0 copy.33
  36.2 0.2 pad.15.q_ref
  36.4 0.0 copy-done.1
  36.4 0.0 copy-start.4
  36.4 0.0 copy-start.2
  36.4 0.0 copy-start.3
  36.5 0.0 copy-start.5
  36.5 32.8 %shard_map.176 = (bf16[256,16,128]{2,1,0:T(8,128)(2,1)S(1)}, bf16[256,128,256]{2,1,0:T(8,128)(2,1)}, bf16[256,128,256]{2,1,0:T(8,128)(2,1)}) custom-call(s32[256]{0:T(256)S(1)} %copy-done.1, bf16[256,16,128]{2,1,0:T(8,128)(2,1)S(1)} %pad.15.q_ref, bf16[16,64,128]{2,1,0:T(8,128)(2,1)S(1)} %pad.16.kn_ref, bf16[16,64,128]{2,1,0:T(8,128)(2,1)S(1)} %pad.17.vn_ref, ...), custom_call_target="tpu_custom_call" | custom-call | flops 1073741824 | bytes 67108864 | tf_op jit(solution)/shard_map/pallas_call | solution.py:75
  69.3 0.0 copy-done
  69.3 0.7 copy.36
  70.0 1.1 copy.37
  71.1 0.0 copy-done.4
  71.1 1.9 %broadcast_in_dim.22.chb_ref = bf16[8,768,128]{2,1,0:T(8,128)(2,1)} broadcast(bf16[8,768]{1,0:T(8,128)(2,1)S(1)} %bitcast.56), dimensions={0,1} | broadcast | bytes 1585152 | tf_op jit(solution)/shard_map/broadcast_in_dim | solution.py:571
  72.9 0.0 copy-done.2
  72.9 0.8 copy.38
  73.7 0.0 copy-done.3
  73.7 0.1 copy.39
  73.8 0.7 pad.18.wr_ref
  74.5 0.0 copy-done.5
  74.5 0.6 reshape.183.g_ref
  75.1 100.2 %shard_map.177 = bf16[3,256,384]{2,1,0:T(8,128)(2,1)} custom-call(bf16[768,384]{1,0:T(8,128)(2,1)} %bitcast.53, bf16[384,384]{1,0:T(8,128)(2,1)} %bitcast.55, bf16[768,384]{1,0:T(8,128)(2,1)} %copy-done, f32[1,384]{1,0:T(1,128)} %reshape.183.g_ref, bf16[384,128]{1,0:T(8,128)(2,1)} %pad.18.wr_ref, bf16[8,768,128]{2,1,0:T(8,128)(2,1)} %broadcast_in_dim.22.chb_ref, ...), custom_call_target="tpu_custom_call" | custom-call | flops 9059696640 | bytes 12582912 | tf_op jit(solution)/shard_map/pallas_call | solution.py:512
  175.3 1.9 %copy.44 = bf16[3,256,384]{2,1,0:T(8,128)(2,1)} copy(bf16[3,256,384]{2,1,0:T(8,128)(2,1)} %shard_map.177) | data formatting | bytes 1179648
  (12 shorter events, 0.2 us)
Async XLA Ops:
  0.6 35.8 %copy-start.1 = (s32[256]{0:T(256)S(1)}, s32[256]{0:T(256)}, u32[]{:S(2)}) copy-start(s32[256]{0:T(256)} %len_ref.1) | copy-start | bytes 3076
  9.4 59.8 %copy-start = (bf16[768,384]{1,0:T(8,128)(2,1)}, bf16[768,384]{1,0:T(8,128)(2,1)S(1)}, u32[]{:S(2)}) copy-start(bf16[768,384]{1,0:T(8,128)(2,1)S(1)} %broadcast_select_fusion.x_ref.xin_ref) | copy-start | bytes 1769476
  36.4 34.6 %copy-start.4 = (s32[3,256,8]{1,2,0:T(8,128)S(1)}, s32[3,256,8]{1,2,0:T(8,128)}, u32[]{:S(2)}) copy-start(s32[3,256,8]{1,2,0:T(8,128)} %param.18) | copy-start | bytes 73732
  36.4 36.5 %copy-start.2 = (bf16[384,384]{1,0:T(8,128)(2,1)S(1)}, bf16[384,384]{1,0:T(8,128)(2,1)}, u32[]{:S(2)}) copy-start(bf16[384,384]{1,0:T(8,128)(2,1)} %param.26) | copy-start | bytes 884740
  36.4 37.3 %copy-start.3 = (bf16[384,40]{0,1:T(8,128)(2,1)S(1)}, bf16[384,40]{0,1:T(8,128)(2,1)}, u32[]{:S(2)}) copy-start(bf16[384,40]{0,1:T(8,128)(2,1)} %param.28) | copy-start | bytes 92164
  36.5 38.0 %copy-start.5 = (bf16[384]{0:T(512)(128)(2,1)S(1)}, bf16[384]{0:T(512)(128)(2,1)}, u32[]{:S(2)}) copy-start(bf16[384]{0:T(512)(128)(2,1)} %param.27) | copy-start | bytes 2308

commit v3 on v2

v3 whole, which is shorter than its diff:
```python
import functools
import jax
import jax.numpy as jnp
from jax import lax
from jax.experimental import pallas as pl
from jax.experimental.pallas import tpu as pltpu
from jax.sharding import PartitionSpec as P

EPS = 1e-5
ROPE_BASE = 1.0e6
MESH = pl.DeviceIdType.MESH
F32 = jnp.float32
BF16 = jnp.bfloat16
LANE = 128
SUB = 16
MIB = 1024 * 1024
LOWEST = -1.0e30
NB = 16
QROWS = 16
HEAD = 64
NEAR = 3


def attn_body(len_ref, q_ref, kn_ref, vn_ref, k_ref, v_ref, o_ref, ko_ref, vo_ref, s_ref, w_ref, qs, ks, vs, os_, *, group):
    half, seq = k_ref.shape[1:]
    steps, n_seq = q_ref.shape[:2]
    step = pl.program_id(0)

    @pl.when(step == 0)
    def _():
        for ref in (qs, ks, vs):
            ref[...] = jnp.zeros_like(ref)

    for t in range(steps):
        ks[pl.ds(t, n_seq, stride=steps), :] = kn_ref[t].astype(F32)
        vs[pl.ds(t, n_seq, stride=steps), :] = vn_ref[t].astype(F32)
        for g in range(group):
            qs[pl.ds(t * group + g, n_seq, stride=QROWS), :] = q_ref[t, :, LANE * g:LANE * (g + 1)].astype(F32)
    kn_t = ks[...].T
    vn_t = vs[...].T
    lane = lax.broadcasted_iota(jnp.int32, (SUB, LANE), 1).astype(F32).astype(BF16)
    srow = lax.broadcasted_iota(jnp.int32, (2 * QROWS, seq), 0)
    scol = lax.broadcasted_iota(jnp.int32, (2 * QROWS, seq), 1)
    srow = jnp.where(srow >= QROWS, srow - QROWS, srow)
    rel = scol - jnp.where(srow >= 2 * group, 2, jnp.where(srow >= group, 1, 0))
    low = lax.broadcasted_iota(jnp.int32, (QROWS, LANE), 1) < HEAD
    low_b = lane < jnp.asarray(HEAD, BF16)
    for b in range(n_seq):
        pos = len_ref[step * n_seq + b]
        turn = lax.rem(pos + LANE - b * steps, LANE)
        new = (pltpu.roll(kn_t, turn, 1).astype(BF16), pltpu.roll(vn_t, turn, 1).astype(BF16))
        gap = lane - jnp.full((SUB, LANE), pos.astype(F32), F32).astype(BF16)
        for tile in range(seq // LANE):
            lo = jnp.asarray(-LANE * tile, BF16)
            hi = jnp.asarray(steps - 1 - LANE * tile, BF16)
            hit = (gap >= lo) & (gap <= hi)
            for i in range(half // SUB):
                rs, cs = slice(SUB * i, SUB * i + SUB), slice(LANE * tile, LANE * tile + LANE)
                ko_ref[b, rs, cs] = jnp.where(hit, new[0][rs], k_ref[b, rs, cs])
                vo_ref[b, rs, cs] = jnp.where(hit, new[1][rs], v_ref[b, rs, cs])
    for b in range(n_seq):
        q16 = qs[QROWS * b:QROWS * (b + 1), :].astype(BF16)
        zero = jnp.zeros_like(q16)
        q32 = jnp.concatenate([jnp.where(low_b, q16, zero), jnp.where(low_b, zero, q16)], axis=0)
        s_ref[b] = jnp.dot(q32, ko_ref[b], preferred_element_type=F32)
    tots = []
    for b in range(n_seq):
        pos = len_ref[step * n_seq + b]
        ok = rel <= pos
        s = jnp.where(ok, s_ref[b] * HEAD ** -0.5, LOWEST)
        peak = jnp.max(s, axis=1, keepdims=True)
        w = jnp.where(ok, jnp.exp(s - peak), 0.0)
        tots.append(jnp.sum(w, axis=1, keepdims=True))
        w_ref[b] = w.astype(BF16)
    for b in range(n_seq):
        o = lax.dot_general(w_ref[b], vo_ref[b], (((1,), (1,)), ((), ())), preferred_element_type=F32)
        o = o / tots[b]
        os_[QROWS * b:QROWS * (b + 1), :] = jnp.where(low, o[:QROWS], o[QROWS:])
    for t in range(steps):
        og = [os_[pl.ds(t * group + g, n_seq, stride=QROWS), :] for g in range(group)]
        turned = pltpu.roll(og[1], HEAD, 1)
        first = low[:n_seq]
        tiles = (jnp.where(first, og[0], turned), jnp.where(first, og[2], og[0]), jnp.where(first, turned, og[2]))
        for g in range(group):
            o_ref[t, :, LANE * g:LANE * (g + 1)] = tiles[g].astype(BF16)


def attention(lengths, proj, kc, vc, group):
    nb, half, seq = kc.shape
    steps = proj.shape[0]
    cache = pl.BlockSpec((NB, half, seq), lambda i, l: (i, 0, 0))
    qs = pl.BlockSpec((steps, NB, group * LANE), lambda i, l: (0, i, 0))
    kspec = pl.BlockSpec((steps, NB, LANE), lambda i, l: (0, i, group))
    vspec = pl.BlockSpec((steps, NB, LANE), lambda i, l: (0, i, group + 1))
    flat = pltpu.VMEM((NB * QROWS, LANE), F32)
    new = pltpu.VMEM((LANE, LANE), F32)
    return pl.pallas_call(
        functools.partial(attn_body, group=group),
        grid_spec=pltpu.PrefetchScalarGridSpec(num_scalar_prefetch=1, grid=(nb // NB,), in_specs=[qs, kspec, vspec, cache, cache], out_specs=[qs, cache, cache],
            scratch_shapes=[pltpu.VMEM((NB, 2 * QROWS, seq), F32), pltpu.VMEM((NB, 2 * QROWS, seq), BF16), flat, new, new, flat]),
        out_shape=[jax.ShapeDtypeStruct((steps, nb, group * LANE), BF16), jax.ShapeDtypeStruct(kc.shape, BF16), jax.ShapeDtypeStruct(vc.shape, BF16)],
        compiler_params=pltpu.CompilerParams(vmem_limit_bytes=40 * MIB, dimension_semantics=("arbitrary",)),
        cost_estimate=pl.CostEstimate(flops=2 * nb * 32 * LANE * seq * 2, bytes_accessed=4 * nb * half * seq * 2, transcendentals=0),
    )(lengths, proj, proj, proj, kc, vc)


def remote(src, dst, ssem, rsem, dev):
    return pltpu.make_async_remote_copy(src_ref=src, dst_ref=dst, send_sem=ssem, recv_sem=rsem, device_id=dev, device_id_type=MESH)


def square_lanes(x_f32):
    acc = x_f32[:, 0:LANE] * x_f32[:, 0:LANE]
    for i in range(1, x_f32.shape[1] // LANE):
        part = x_f32[:, LANE * i:LANE * (i + 1)]
        acc = acc + part * part
    return acc


def square_rows(x_f32):
    return jnp.sum(square_lanes(x_f32).T, axis=0, keepdims=True)


def scale_rows(x_f32, stat_row, gain, width_full):
    scale = lax.rsqrt(stat_row / width_full + EPS)
    col = jnp.broadcast_to(scale, (LANE, LANE)).T
    parts = [x_f32[:, LANE * i:LANE * (i + 1)] * col * gain[:, LANE * i:LANE * (i + 1)] for i in range(x_f32.shape[1] // LANE)]
    return jnp.concatenate(parts, axis=1).astype(BF16)


def front_body(x_ref, g_ref, wq_ref, wk_ref, wv_ref, cos_ref, sin_ref, out_ref, st, st_in, hh, pj, rs1, cs, rs2, sts, str_, s1s, s1r, s2s, s2r, s3s, s3r, *, width_full):
    steps, nb = out_ref.shape[:2]
    q_cols, k_cols = wq_ref.shape[1], wk_ref.shape[1]
    gain = g_ref[0:1, :]
    cols = out_ref.shape[2]
    hb = nb // 2
    dp, y, x = lax.axis_index("dp"), lax.axis_index("y"), lax.axis_index("x")
    core, chip = x % 2, x // 2
    sib = (dp, y, chip * 2 + (1 - core))
    peer = (dp, y, (1 - chip) * 2 + core)
    diag = (dp, y, (1 - chip) * 2 + (1 - core))
    near = (sib, peer, diag)
    barrier = pltpu.get_barrier_semaphore()
    for dev in near:
        pl.semaphore_signal(barrier, inc=1, device_id=dev, device_id_type=MESH)
    keep = pl.multiple_of(core * hb, hb)
    give = pl.multiple_of((1 - core) * hb, hb)
    st[...] = jnp.zeros_like(st)
    blocks = steps * nb // LANE
    for i in range(blocks):
        st[i:i + 1, :] = square_rows(x_ref[LANE * i:LANE * (i + 1), :].astype(F32))
    pl.semaphore_wait(barrier, 3)
    stat = [remote(st, st_in.at[k], sts.at[k], str_.at[k], near[k]) for k in range(3)]
    for k in range(3):
        stat[k].start()
    for k in range(3):
        stat[k].wait_recv()
    total = st[...] + st_in[0] + st_in[1] + st_in[2]

    def s1(c):
        return remote(pj.at[c, pl.ds(give, hb), :], rs1.at[c], s1s.at[c], s1r.at[c], sib)

    def s2(c):
        return remote(cs.at[c], rs2.at[c], s2s.at[c], s2r.at[c], peer)

    def s3(c, row):
        return remote(out_ref.at[c, pl.ds(row, hb), :], out_ref.at[c, pl.ds(row, hb), :], s3s.at[c], s3r.at[c], sib)

    def mid(c):
        s1(c).wait_recv()
        cs[c] = (pj[c, pl.ds(keep, hb), :].astype(F32) + rs1[c].astype(F32)).astype(BF16)
        s2(c).start()

    def last(c):
        s2(c).wait_recv()
        fin = (cs[c].astype(F32) + rs2[c].astype(F32)).astype(BF16).astype(F32)
        cosv = cos_ref[c, pl.ds(keep, hb), :]
        sinv = sin_ref[c, pl.ds(keep, hb), :]
        lane = lax.broadcasted_iota(jnp.int32, (hb, LANE), 1)
        first, low = lane % HEAD < HEAD // 2, lane < HEAD
        tiles = [fin[:, LANE * i:LANE * (i + 1)] for i in range(cols // LANE)]
        for i in range((q_cols + k_cols) // LANE):
            v = tiles[i]
            swap = jnp.where(first, pltpu.roll(v, LANE - HEAD // 2, 1), pltpu.roll(v, HEAD // 2, 1))
            tiles[i] = v * cosv + swap * sinv
        ta, tb, tc = tiles[:NEAR]
        tiles[:NEAR] = [jnp.where(low, ta, tb), pltpu.roll(jnp.where(low, tc, ta), HEAD, 1), jnp.where(low, tb, tc)]
        for i in range(cols // LANE):
            out_ref[c, pl.ds(keep, hb), LANE * i:LANE * (i + 1)] = tiles[i].astype(BF16)
        s3(c, keep).start()

    for c in range(steps):
        for i in range(c * nb // LANE, (c + 1) * nb // LANE):
            hh[LANE * i:LANE * (i + 1), :] = scale_rows(x_ref[LANE * i:LANE * (i + 1), :].astype(F32), total[i:i + 1, :], gain, width_full)
        normed = hh[c * nb:(c + 1) * nb, :]
        pj[c, :, 0:q_cols] = jnp.dot(normed, wq_ref[...], preferred_element_type=F32).astype(BF16)
        pj[c, :, q_cols:q_cols + k_cols] = jnp.dot(normed, wk_ref[...], preferred_element_type=F32).astype(BF16)
        pj[c, :, q_cols + k_cols:cols] = jnp.dot(normed, wv_ref[...], preferred_element_type=F32).astype(BF16)
        s1(c).start()
        if c >= 1:
            mid(c - 1)
    mid(steps - 1)
    for c in range(steps):
        last(c)
    for c in range(steps):
        s3(c, give).wait_recv()
    for k in range(3):
        stat[k].wait_send()
    for c in range(steps):
        s1(c).wait_send()
        s2(c).wait_send()
        s3(c, keep).wait_send()


def front(x_in, gain, w_q, w_k, w_v, cosv, sinv, steps, width_full):
    rows, width = x_in.shape
    nb = rows // steps
    cols = w_q.shape[1] + 2 * w_k.shape[1]
    hb = nb // 2
    dma = pltpu.SemaphoreType.DMA
    vm = pl.BlockSpec(memory_space=pltpu.VMEM)
    return pl.pallas_call(
        functools.partial(front_body, width_full=width_full),
        out_shape=jax.ShapeDtypeStruct((steps, nb, cols), BF16),
        in_specs=[vm] * 7,
        out_specs=vm,
        scratch_shapes=[
            pltpu.VMEM((8, LANE), F32), pltpu.VMEM((3, 8, LANE), F32),
            pltpu.VMEM((rows, width), BF16), pltpu.VMEM((steps, nb, cols), BF16),
            pltpu.VMEM((steps, hb, cols), BF16), pltpu.VMEM((steps, hb, cols), BF16), pltpu.VMEM((steps, hb, cols), BF16),
            dma((3,)), dma((3,)), dma((steps,)), dma((steps,)), dma((steps,)), dma((steps,)), dma((steps,)), dma((steps,)),
        ],
        compiler_params=pltpu.CompilerParams(collective_id=2, has_side_effects=True, vmem_limit_bytes=24 * MIB),
        cost_estimate=pl.CostEstimate(flops=2 * rows * width * cols, bytes_accessed=4 * MIB, transcendentals=0),
    )(x_in, gain, w_q, w_k, w_v, cosv, sinv)


def tail_body(mix_ref, wo_ref, xin_ref, g_ref, wr_ref, ch_ref, wact_hbm, wlin_hbm, wdn_hbm, out_ref,
              wcat, wdn, pa, ar, xm, hh, st, st_in, hs, rs1, cs, rs2, lgp, lr1, lcs, lr2, u, pd, yr,
              wsem, as_, ar_s, xs, xr, sts, str_, s1s, s1r, s2s, s2r, l1s, l1r, l2s, l2r, us, ur, ys, yrs, gs, gr, *, width_full):
    experts = wcat.shape[0]
    ff = wact_hbm.shape[2]
    steps, top, nb = ch_ref.shape
    parts = rs1.shape[0]
    per = parts // steps
    ns = nb // per
    hb, qb = ns // 2, ns // 4
    dp, y, x = lax.axis_index("dp"), lax.axis_index("y"), lax.axis_index("x")
    core, chip = x % 2, x // 2
    sib = (dp, y, chip * 2 + (1 - core))
    peer = (dp, y, (1 - chip) * 2 + core)
    diag = (dp, y, (1 - chip) * 2 + (1 - core))
    near = (sib, peer, diag)
    hops = range(1, NEAR + 1)
    ypeer = [None] + [(dp, (y + d) % (NEAR + 1), x) for d in hops]
    slots = range(NEAR)
    nothing = (((1,), (1,)), ((), ()))

    w0 = pltpu.make_async_copy(wact_hbm, wcat.at[:, :, pl.ds(0, ff)], wsem.at[0])
    w1 = pltpu.make_async_copy(wlin_hbm, wcat.at[:, :, pl.ds(ff, ff)], wsem.at[1])
    w2 = pltpu.make_async_copy(wdn_hbm, wdn, wsem.at[2])
    barrier = pltpu.get_barrier_semaphore()
    for dev in near + tuple(ypeer[1:]):
        pl.semaphore_signal(barrier, inc=1, device_id=dev, device_id_type=MESH)

    def rows(k, start, size):
        return pl.ds(pl.multiple_of(k * ns + start, SUB), size)

    keep, give = core * hb, (1 - core) * hb
    sub_keep, sub_give = chip * qb, (1 - chip) * qb
    own, other = keep + sub_keep, keep + sub_give
    sib_own, sib_other = give + sub_keep, give + sub_give

    def ydist(d):
        return ((y + d) % (NEAR + 1)) * qb

    def rs_send(buf, land, ssem, rsem, k, d):
        return remote(buf.at[rows(k, ydist(d), qb), :], land.at[k, NEAR - d], ssem.at[k, d - 1], rsem.at[k, NEAR - d], ypeer[d])

    def rs_recv(buf, land, ssem, rsem, k, i):
        return remote(buf.at[rows(k, 0, qb), :], land.at[k, i], ssem.at[k, i], rsem.at[k, i], ypeer[1])

    def ag_send(buf, ssem, rsem, k, d):
        mine = buf.at[rows(k, y * qb, qb), :]
        return remote(mine, mine, ssem.at[k, d - 1], rsem.at[k, NEAR - d], ypeer[d])

    def ag_recv(buf, ssem, rsem, k, i):
        theirs = buf.at[rows(k, ydist(i + 1), qb), :]
        return remote(theirs, theirs, ssem.at[k, i], rsem.at[k, i], ypeer[1])

    def s1(k):
        return remote(hs.at[rows(k, give, hb), :], rs1.at[k], s1s.at[k], s1r.at[k], sib)

    def s2(k):
        return remote(cs.at[k], rs2.at[k], s2s.at[k], s2r.at[k], peer)

    def l1(k):
        return remote(lgp.at[rows(k, give, hb), :], lr1.at[k], l1s.at[k], l1r.at[k], sib)

    def l2(k):
        return remote(lcs.at[k], lr2.at[k], l2s.at[k], l2r.at[k], peer)

    def u_copy(k, row, i):
        blk = u.at[rows(k, row, qb), :]
        return remote(blk, blk, us.at[k, i], ur.at[k, i], peer if i == 0 else sib)

    def stat(k, i):
        return remote(st.at[k], st_in.at[k, i], sts.at[k, i], str_.at[k, i], near[i])

    def attn_out(c):
        pa[c * nb:(c + 1) * nb, :] = jnp.dot(mix_ref[c], wo_ref[...], preferred_element_type=F32).astype(BF16)

    def attn_send(k):
        for d in hops:
            rs_send(pa, ar, as_, ar_s, k, d).start()

    def attn_sum(k):
        for i in slots:
            rs_recv(pa, ar, as_, ar_s, k, i).wait_recv()
        acc = pa[rows(k, y * qb, qb), :].astype(F32)
        for i in slots:
            acc = acc + ar[k, i].astype(F32)
        mid = (xin_ref[rows(k, y * qb, qb), :].astype(F32) + acc).astype(BF16)
        xm[k] = mid
        st[k] = square_lanes(mid.astype(F32))
        for i in slots:
            stat(k, i).start()

    def norm(k):
        for i in slots:
            stat(k, i).wait_recv()
        total = st[k]
        for i in slots:
            total = total + st_in[k, i]
        scale = lax.rsqrt(jnp.sum(total, axis=1, keepdims=True) / width_full + EPS)
        hh[rows(k, y * qb, qb), :] = (xm[k].astype(F32) * scale * g_ref[1:2, :]).astype(BF16)
        for d in hops:
            ag_send(hh, xs, xr, k, d).start()

    def ready(c):
        for k in range(c * per, (c + 1) * per):
            for i in slots:
                ag_recv(hh, xs, xr, k, i).wait_recv()
        blk = slice(c * nb, (c + 1) * nb)
        lgp[blk, 0:experts] = lax.dot_general(hh[blk, :], wr_ref[...], nothing, preferred_element_type=F32)
        for k in range(c * per, (c + 1) * per):
            l1(k).start()

    def experts_in(c, part, hd):
        span = 4
        half = experts // span // 2

        def few(i, carry):
            for q in range(span):
                e = i * span + q
                hval = jnp.dot(hh[c * nb:(c + 1) * nb, :], wcat[e], preferred_element_type=F32)
                hd[e] = hval[:, 0:ff].astype(BF16)
                hd[experts + e] = hval[:, ff:2 * ff].astype(BF16)
            return carry
        lax.fori_loop(part * half, (part + 1) * half, few, 0)

    def pick(k, hd, chs):
        def tile(i, carry):
            r = pl.multiple_of((k % per) * ns + i * SUB, SUB)
            ch = [chs[j, rows(k, i * SUB, SUB), :] for j in range(top)]
            span = 8

            def some(g, state):
                acc, ev = list(state[0]), state[1]
                for q in range(span):
                    e = g * span + q
                    va = hd[e, pl.ds(r, SUB), :]
                    vl = hd[experts + e, pl.ds(r, SUB), :]
                    for j in range(top):
                        m = ch[j] == ev
                        acc[2 * j] = jnp.where(m, va, acc[2 * j])
                        acc[2 * j + 1] = jnp.where(m, vl, acc[2 * j + 1])
                    ev = ev + jnp.ones_like(ev)
                return tuple(acc), ev
            zero = jnp.zeros((SUB, ff), BF16)
            acc, _ = lax.fori_loop(0, experts // span, some, (tuple(zero for _ in range(2 * top)), zero))
            for q in range(2 * top):
                hs[rows(k, i * SUB, SUB), q * ff:(q + 1) * ff] = acc[q]
            return carry
        lax.fori_loop(0, ns // SUB, tile, 0)
        s1(k).start()

    def logits_mid(k):
        l1(k).wait_recv()
        lcs[k] = lgp[rows(k, other, qb), :] + lr1[k, pl.ds(pl.multiple_of(sub_give, SUB), qb), :]
        l2(k).start()

    def part_b(k):
        logits_mid(k)
        s1(k).wait_recv()

        def add(i, carry):
            mine = hs[rows(k, other + i * SUB, SUB), :].astype(F32)
            got = rs1[k, pl.ds(pl.multiple_of(sub_give + i * SUB, SUB), SUB), :].astype(F32)
            cs[k, pl.ds(pl.multiple_of(i * SUB, SUB), SUB), :] = (mine + got).astype(BF16)
            return carry
        lax.fori_loop(0, qb // SUB, add, 0)
        s2(k).start()

    def part_u(k, chs):
        l2(k).wait_recv()
        s2(k).wait_recv()

        def tile(i, carry):
            r = pl.ds(pl.multiple_of(i * SUB, SUB), SUB)
            r_own = rows(k, own + i * SUB, SUB)
            r_sub = pl.ds(pl.multiple_of(sub_keep + i * SUB, SUB), SUB)
            logit = lgp[r_own, :] + lr1[k, r_sub, :] + lr2[k, r, :]
            lane = lax.broadcasted_iota(jnp.int32, (SUB, LANE), 1).astype(F32)
            hit = [chs[j, r_own, :].astype(F32) == lane for j in range(top)]
            any_hit = hit[0]
            for j in range(1, top):
                any_hit = any_hit | hit[j]
            peak = jnp.max(jnp.where(any_hit, logit, -jnp.inf), axis=1, keepdims=True)
            ex = jnp.where(any_hit, jnp.exp(logit - peak), 0.0)
            coef = ex / jnp.sum(ex, axis=1, keepdims=True)
            for j in range(top):
                gate = jnp.sum(jnp.where(hit[j], coef, 0.0), axis=1, keepdims=True)
                ca, cl = pl.ds(2 * j * ff, ff), pl.ds((2 * j + 1) * ff, ff)
                act = hs[r_own, ca].astype(F32) + rs1[k, r_sub, ca].astype(F32) + rs2[k, r, ca].astype(F32)
                lin = hs[r_own, cl].astype(F32) + rs1[k, r_sub, cl].astype(F32) + rs2[k, r, cl].astype(F32)
                val = gate * (act / (1.0 + jnp.exp(-act))) * lin
                u[r_own, j * ff:(j + 1) * ff] = val.astype(BF16)
            return carry
        lax.fori_loop(0, qb // SUB, tile, 0)
        u_copy(k, own, 0).start()
        u_copy(k, own, 1).start()

    def part_f(k):
        u_copy(k, other, 0).wait_recv()
        u_copy(k, other, 2).start()

    def part_d(k, ud, chs, us16):
        u_copy(k, sib_own, 1).wait_recv()
        u_copy(k, sib_other, 2).wait_recv()
        for j in range(top):
            us16[j] = u[k * ns:(k + 1) * ns, j * ff:(j + 1) * ff]

        def spread(i, carry):
            r = pl.ds(pl.multiple_of(i * SUB, SUB), SUB)
            ch = [chs[j, rows(k, i * SUB, SUB), :] for j in range(top)]
            vals = [us16[j, r, :] for j in range(top)]
            for e in range(experts):
                acc = jnp.zeros((SUB, ff), BF16)
                for j in range(top):
                    acc = jnp.where(ch[j] == jnp.asarray(e, BF16), vals[j], acc)
                ud[r, e * ff:(e + 1) * ff] = acc
            return carry
        lax.fori_loop(0, ns // SUB, spread, 0)
        pd[k * ns:(k + 1) * ns, :] = jnp.dot(ud[...], wdn[...], preferred_element_type=F32).astype(BF16)
        for d in hops:
            rs_send(pd, yr, ys, yrs, k, d).start()

    def part_g(k):
        for i in slots:
            rs_recv(pd, yr, ys, yrs, k, i).wait_recv()
        acc = pd[rows(k, y * qb, qb), :].astype(F32)
        for i in slots:
            acc = acc + yr[k, i].astype(F32)
        out_ref[rows(k, y * qb, qb), :] = (xm[k].astype(F32) + acc).astype(BF16)
        for d in hops:
            ag_send(out_ref, gs, gr, k, d).start()

    def run(hd, ud, chs, us16):
        w0.start()
        w1.start()
        w2.start()
        for c in range(steps):
            attn_out(c)
        lgp[...] = jnp.zeros_like(lgp)
        for c in range(steps):
            for i in range(nb // LANE):
                for j in range(top):
                    row = ch_ref[c, j:j + 1, LANE * i:LANE * (i + 1)].astype(F32)
                    chs[j, c * nb + LANE * i:c * nb + LANE * (i + 1), :] = jnp.broadcast_to(row, (LANE, LANE)).T.astype(BF16)
        pl.semaphore_wait(barrier, 2 * NEAR)
        attn_send(0)
        attn_send(1)
        attn_sum(0)
        attn_sum(1)
        norm(0)
        norm(1)
        attn_send(2)
        attn_send(3)
        ready(0)
        w0.wait()
        w1.wait()
        experts_in(0, 0, hd)
        attn_sum(2)
        attn_sum(3)
        experts_in(0, 1, hd)
        norm(2)
        norm(3)
        attn_send(4)
        attn_send(5)
        pick(0, hd, chs)
        pick(1, hd, chs)
        part_b(0)
        part_b(1)
        ready(1)
        experts_in(1, 0, hd)
        attn_sum(4)
        attn_sum(5)
        experts_in(1, 1, hd)
        norm(4)
        norm(5)
        part_u(0, chs)
        pick(2, hd, chs)
        part_u(1, chs)
        pick(3, hd, chs)
        part_b(2)
        part_f(0)
        part_b(3)
        part_f(1)
        w2.wait()
        part_d(0, ud, chs, us16)
        ready(2)
        experts_in(2, 0, hd)
        part_d(1, ud, chs, us16)
        experts_in(2, 1, hd)
        part_u(2, chs)
        pick(4, hd, chs)
        part_u(3, chs)
        pick(5, hd, chs)
        part_b(4)
        part_f(2)
        part_b(5)
        part_f(3)
        part_g(0)
        part_d(2, ud, chs, us16)
        part_g(1)
        part_u(4, chs)
        part_d(3, ud, chs, us16)
        part_u(5, chs)
        part_f(4)
        part_g(2)
        part_d(4, ud, chs, us16)
        part_f(5)
        part_g(3)
        part_d(5, ud, chs, us16)
        part_g(4)
        part_g(5)

    bf = functools.partial(pltpu.VMEM, dtype=BF16)
    pl.run_scoped(run, bf((2 * experts, nb, ff)), bf((ns, experts * ff)), bf((top, steps * nb, ff)), bf((top, ns, ff)))

    for k in range(parts):
        for i in slots:
            ag_recv(out_ref, gs, gr, k, i).wait_recv()
    for k in range(parts):
        for i in slots:
            stat(k, i).wait_send()
        l1(k).wait_send()
        l2(k).wait_send()
        s1(k).wait_send()
        s2(k).wait_send()
        u_copy(k, own, 0).wait_send()
        u_copy(k, own, 1).wait_send()
        u_copy(k, other, 2).wait_send()
        for d in hops:
            rs_send(pa, ar, as_, ar_s, k, d).wait_send()
            ag_send(hh, xs, xr, k, d).wait_send()
            rs_send(pd, yr, ys, yrs, k, d).wait_send()
            ag_send(out_ref, gs, gr, k, d).wait_send()


def tail(mixed, wo, x_in, gain, w_router, chosen, w_act, w_lin, w_down, width_full):
    total, width = x_in.shape
    steps, top, nb = chosen.shape
    experts, _, ff = w_act.shape
    parts = 2 * steps
    ns = nb // 2
    hb, qb = ns // 2, ns // 4
    dma = pltpu.SemaphoreType.DMA
    vm = pl.BlockSpec(memory_space=pltpu.VMEM)
    hbm = pl.BlockSpec(memory_space=pl.ANY)
    bf = functools.partial(pltpu.VMEM, dtype=BF16)
    fl = functools.partial(pltpu.VMEM, dtype=F32)
    wide = 2 * top * ff
    each, three = (parts,), (parts, NEAR)
    sems = [three] * 6 + [each] * 8 + [three] * 6
    return pl.pallas_call(
        functools.partial(tail_body, width_full=width_full),
        out_shape=jax.ShapeDtypeStruct((total, width), BF16),
        in_specs=[vm] * 6 + [hbm] * 3,
        out_specs=vm,
        scratch_shapes=[
            bf((experts, width, 2 * ff)), bf((experts * ff, width)),
            bf((total, width)), bf((parts, NEAR, qb, width)), bf((parts, qb, width)), bf((total, width)),
            fl((parts, qb, LANE)), fl((parts, NEAR, qb, LANE)),
            bf((total, wide)), bf((parts, hb, wide)), bf((parts, qb, wide)), bf((parts, qb, wide)),
            fl((total, LANE)), fl((parts, hb, LANE)), fl((parts, qb, LANE)), fl((parts, qb, LANE)),
            bf((total, top * ff)), bf((total, width)), bf((parts, NEAR, qb, width)),
            dma((NEAR,)),
        ] + [dma(n) for n in sems],
        compiler_params=pltpu.CompilerParams(collective_id=1, has_side_effects=True, vmem_limit_bytes=60 * MIB),
        cost_estimate=pl.CostEstimate(flops=6 * total * width * experts * ff, bytes_accessed=12 * MIB, transcendentals=0),
    )(mixed, wo, x_in, gain, w_router, chosen, w_act, w_lin, w_down.reshape(experts * ff, width))


def turn_tables(positions, head_dim):
    half_dim = head_dim // 2
    inv_freq = ROPE_BASE ** (-(jnp.arange(half_dim, dtype=F32) * 2.0 / head_dim))
    angles = positions.astype(F32)[:, None] * inv_freq[None, :]
    cosine, sine_val = jnp.cos(angles), jnp.sin(angles)
    return jnp.tile(cosine, (1, 4)), jnp.tile(jnp.concatenate([-sine_val, sine_val], axis=1), (1, 2))


def solution(mesh):
    x_count = mesh.shape['x']
    cache_spec = P('dp', None, 'y', None)
    in_specs = (P(None, 'dp'), P('dp'), P(None, 'dp', None), P(None, 'x'), cache_spec, cache_spec, P('x'), P('x', 'y'), P('x', 'y'), P('x', 'y'), P('y', 'x'), P('x'), P('x', None), P(None, 'x', 'y'), P(None, 'x', 'y'), P(None, 'y', 'x'))
    out_specs = (P(None, 'dp', 'x'), cache_spec, cache_spec)

    def per_device(tokens, lengths, choices, emb_table, k_cache, v_cache, g_attn, w_q, w_k, w_v, w_o, g_ffn, w_router, w_act, w_lin, w_down):
        steps, nb = tokens.shape
        seq, kvl, hdim = k_cache.shape[1:]
        q_cols, kv_cols = w_q.shape[1], w_k.shape[1]
        width = emb_table.shape[1]
        width_full = width * x_count
        group = q_cols // kv_cols
        rows = steps * nb
        positions = (lengths[None, :] + jnp.arange(steps, dtype=lengths.dtype)[:, None]).reshape(rows)
        cosv, sinv = turn_tables(positions, hdim)
        x_in = emb_table.at[tokens].get(mode="promise_in_bounds").reshape(rows, width)
        first = lax.broadcasted_iota(jnp.int32, (2, width), 0) == 0
        gains = jnp.where(first, g_attn[None, :], g_ffn[None, :]).astype(F32)
        proj = front(x_in, gains, w_q, w_k, w_v, cosv.reshape(steps, nb, LANE), sinv.reshape(steps, nb, LANE), steps, width_full)
        kc = k_cache.transpose(0, 2, 3, 1).reshape(nb, kv_cols, seq)
        vc = v_cache.transpose(0, 2, 3, 1).reshape(nb, kv_cols, seq)
        mixed, ko, vo = attention(lengths, proj, kc, vc, group)
        hidden = tail(mixed, w_o, x_in, gains, w_router.T, choices.transpose(0, 2, 1), w_act, w_lin, w_down, width_full).reshape(steps, nb, width)
        ko = ko.reshape(nb, kvl, hdim, seq).transpose(0, 3, 1, 2)
        vo = vo.reshape(nb, kvl, hdim, seq).transpose(0, 3, 1, 2)
        return hidden, ko, vo

    return jax.shard_map(per_device, mesh=mesh, in_specs=in_specs, out_specs=out_specs, check_vma=False)
```

time: 178 us -> 157 us (0.88)
  Pallas kernels: 154 us -> 141 us
  local copies, waits for them, and re-layouts: 19.6 us -> 12.1 us
    pallas_call x1, Pallas kernels: 100 us -> 87.2 us  [tail(): pl.pallas_call(functools.partial(tail_body, width_full=width_full), out_s...]
    reshape x8 -> x0, local copies, waits for them, and re-layouts: 4.25 us -> none  [the longest x1 1 us: per_device(): proj[:, :, :q_cols].reshape(steps, nb, group, kv_cols).transpose(1, 0, 2, 3)]
    unnamed x16 -> x15, local copies, waits for them, and re-layouts: 4.18 us -> 6.17 us
    broadcast_in_dim x1, local copies, waits for them, and re-layouts: 1.86 us -> 0.01 us  [per_device(): emb_table.at[tokens].get(mode='promise_in_bounds').reshape(rows, width)]
where the time goes in v3:
time: 157 us; the launch traced here: 156 us
  Pallas kernels  141 us (90%)
  local copies, waits for them, and re-layouts  12.1 us (8%)
  other arithmetic  2.62 us (2%)
    pallas_call x1, Pallas kernels, tail(): pl.pallas_call(functools.partial(tail_body, width_full=width_full), out_s...  87.2 us
    pallas_call x1, Pallas kernels, attention(): pl.pallas_call(functools.partial(attn_body, group=group), grid_spec=pltpu...  32.2 us
    pallas_call x1, Pallas kernels, front(): pl.pallas_call(functools.partial(front_body, width_full=width_full), out_...  21.4 us
    unnamed x15, local copies, waits for them, and re-layouts  6.17 us
    gather x1, local copies, waits for them, and re-layouts, per_device(): emb_table.at[tokens].get(mode='promise_in_bounds').reshape(rows, width)  5.01 us

profile of v3, /device:TPU:0, one launch (start us, length us, event | category | flops | bytes accessed | tf_op | source)
XLA Modules:
  0.0 156.3 jit_solution(7223013691325219837)
XLA Ops:
  0.7 0.8 fusion.1.g_ref
  1.4 0.0 copy-start.4
  1.4 0.7 compare_select_fusion
  2.1 0.7 add_convert_fusion
  2.8 0.4 fusion
  3.3 0.2 tile.19
  3.5 0.2 copy.20.sin_ref
  3.8 0.2 tile.17
  4.0 0.2 copy.19.cos_ref
  4.2 5.0 %gather_fusion = bf16[768,384]{1,0:T(8,128)(2,1)S(1)} fusion(bf16[49152,384]{1,0:T(8,128)(2,1)} %param.19, s32[1024]{0:T(1024)S(1)} %pad_clamp_fusion), kind=kCustom, calls=%fused_computation | custom fusion | bytes 1182720 | tf_op jit(solution)/shard_map/gather | solution.py:629
  9.2 0.0 copy-start.1
  9.2 1.0 copy-done.1
  10.2 0.0 copy-start.2
  10.2 0.9 copy-done.2
  11.1 0.0 copy-start.3
  11.1 0.9 copy-done.3
  12.0 0.0 copy-start
  12.0 21.4 %shard_map.175.q_ref.kn_ref.vn_ref = bf16[3,256,640]{2,1,0:T(8,128)(2,1)S(1)} custom-call(bf16[768,384]{1,0:T(8,128)(2,1)S(1)} %gather_fusion, f32[2,384]{1,0:T(2,128)S(1)} %fusion.1.g_ref, bf16[384,384]{1,0:T(8,128)(2,1)S(1)} %copy-done.1, bf16[384,128]{1,0:T(8,128)(2,1)S(1)} %copy-done.2, bf16[384,128]{1,0:T(8,128)(2,1)S(1)} %copy-done.3, ...), custom_call_target="tpu_custom_call" | custom-call | flops 377487360 | bytes 4194304 | tf_op jit(solution)/shard_map/pallas_call | solution.py:221
  33.4 0.0 copy-start.5
  33.4 0.7 copy-done.5
  34.1 32.2 %shard_map.176 = (bf16[3,256,384]{2,1,0:T(8,128)(2,1)S(1)}, bf16[256,128,256]{2,1,0:T(8,128)(2,1)}, bf16[256,128,256]{2,1,0:T(8,128)(2,1)}) custom-call(s32[256]{0:T(256)S(1)} %copy-done.5, bf16[3,256,640]{2,1,0:T(8,128)(2,1)S(1)} %shard_map.175.q_ref.kn_ref.vn_ref, bf16[3,256,640]{2,1,0:T(8,128)(2,1)S(1)} %shard_map.175.q_ref.kn_ref.vn_ref, ...), custom_call_target="tpu_custom_call" | custom-call | flops 1073741824 | bytes 67108864 | tf_op jit(solution)/shard_map/pallas_call | solution.py:97
  66.3 0.0 copy-done.4
  66.3 0.0 copy-done
  66.3 0.0 copy-start.6
  66.3 0.8 copy-done.6
  67.1 87.2 %shard_map.177 = bf16[768,384]{1,0:T(8,128)(2,1)} custom-call(bf16[3,256,384]{2,1,0:T(8,128)(2,1)} %copy-done.6, bf16[384,384]{1,0:T(8,128)(2,1)} %wo_ref.1, bf16[768,384]{1,0:T(8,128)(2,1)} %copy-done, f32[2,384]{1,0:T(2,128)} %copy-done.4, bf16[40,384]{1,0:T(8,128)(2,1)} %bitcast.26, s32[3,8,256]{2,1,0:T(8,128)} %bitcast.27, ...), custom_call_target="tpu_custom_call" | custom-call | flops 9059696640 | bytes 12582912 | tf_op jit(solution)/shard_map/pallas_call | solution.py:586
  154.4 1.9 %copy.22 = bf16[3,256,384]{2,1,0:T(8,128)(2,1)} copy(bf16[3,256,384]{2,1,0:T(8,128)(2,1)} %bitcast.22) | data formatting | bytes 1179648
  (8 shorter events, 0.1 us)
Async XLA Ops:
  1.4 64.9 %copy-start.4 = (f32[2,384]{1,0:T(2,128)}, f32[2,384]{1,0:T(2,128)S(1)}, u32[]{:S(2)}) copy-start(f32[2,384]{1,0:T(2,128)S(1)} %fusion.1.g_ref) | copy-start | bytes 9220
  9.2 1.0 copy-start.1
  10.2 0.9 copy-start.2
  11.1 0.9 copy-start.3
  12.0 54.3 %copy-start = (bf16[768,384]{1,0:T(8,128)(2,1)}, bf16[768,384]{1,0:T(8,128)(2,1)S(1)}, u32[]{:S(2)}) copy-start(bf16[768,384]{1,0:T(8,128)(2,1)S(1)} %gather_fusion) | copy-start | bytes 1769476
  33.4 0.7 copy-start.5
  66.3 0.8 copy-start.6

commit v4 on v3

--- a/solution.py
+++ b/solution.py
@@ -15,7 +15,7 @@
 SUB = 16
 MIB = 1024 * 1024
 LOWEST = -1.0e30
-NB = 16
+NB = 32
 QROWS = 16
 HEAD = 64
 NEAR = 3
@@ -79,7 +79,7 @@
     for t in range(steps):
         og = [os_[pl.ds(t * group + g, n_seq, stride=QROWS), :] for g in range(group)]
         turned = pltpu.roll(og[1], HEAD, 1)
-        first = low[:n_seq]
+        first = lax.broadcasted_iota(jnp.int32, (n_seq, LANE), 1) < HEAD
         tiles = (jnp.where(first, og[0], turned), jnp.where(first, og[2], og[0]), jnp.where(first, turned, og[2]))
         for g in range(group):
             o_ref[t, :, LANE * g:LANE * (g + 1)] = tiles[g].astype(BF16)
@@ -99,7 +99,7 @@
         grid_spec=pltpu.PrefetchScalarGridSpec(num_scalar_prefetch=1, grid=(nb // NB,), in_specs=[qs, kspec, vspec, cache, cache], out_specs=[qs, cache, cache],
             scratch_shapes=[pltpu.VMEM((NB, 2 * QROWS, seq), F32), pltpu.VMEM((NB, 2 * QROWS, seq), BF16), flat, new, new, flat]),
         out_shape=[jax.ShapeDtypeStruct((steps, nb, group * LANE), BF16), jax.ShapeDtypeStruct(kc.shape, BF16), jax.ShapeDtypeStruct(vc.shape, BF16)],
-        compiler_params=pltpu.CompilerParams(vmem_limit_bytes=40 * MIB, dimension_semantics=("arbitrary",)),
+        compiler_params=pltpu.CompilerParams(vmem_limit_bytes=60 * MIB, dimension_semantics=("arbitrary",)),
         cost_estimate=pl.CostEstimate(flops=2 * nb * 32 * LANE * seq * 2, bytes_accessed=4 * nb * half * seq * 2, transcendentals=0),
     )(lengths, proj, proj, proj, kc, vc)
 
@@ -127,7 +127,7 @@
     return jnp.concatenate(parts, axis=1).astype(BF16)
 
 
-def front_body(x_ref, g_ref, wq_ref, wk_ref, wv_ref, cos_ref, sin_ref, out_ref, st, st_in, hh, pj, rs1, cs, rs2, sts, str_, s1s, s1r, s2s, s2r, s3s, s3r, *, width_full):
+def front_body(x_ref, g_ref, wq_ref, wk_ref, wv_ref, out_ref, st, st_in, hh, pj, rs1, cs, rs2, sts, str_, s1s, s1r, s2s, s2r, s3s, s3r, *, width_full):
     steps, nb = out_ref.shape[:2]
     q_cols, k_cols = wq_ref.shape[1], wk_ref.shape[1]
     gain = g_ref[0:1, :]
@@ -171,12 +171,15 @@
         s2(c).start()
 
     def last(c):
+        lane = lax.broadcasted_iota(jnp.int32, (hb, LANE), 1)
+        inv_freq = ROPE_BASE ** (-((lane % (HEAD // 2)).astype(F32) * 2.0 / HEAD))
+        length = jnp.broadcast_to(g_ref[2:3, pl.ds(keep, hb)], (LANE, hb)).T
+        angle = (length + float(c)) * inv_freq
+        first, low = lane % HEAD < HEAD // 2, lane < HEAD
+        cosv, sinv = jnp.cos(angle), jnp.sin(angle)
+        sinv = jnp.where(first, -sinv, sinv)
         s2(c).wait_recv()
         fin = (cs[c].astype(F32) + rs2[c].astype(F32)).astype(BF16).astype(F32)
-        cosv = cos_ref[c, pl.ds(keep, hb), :]
-        sinv = sin_ref[c, pl.ds(keep, hb), :]
-        lane = lax.broadcasted_iota(jnp.int32, (hb, LANE), 1)
-        first, low = lane % HEAD < HEAD // 2, lane < HEAD
         tiles = [fin[:, LANE * i:LANE * (i + 1)] for i in range(cols // LANE)]
         for i in range((q_cols + k_cols) // LANE):
             v = tiles[i]
@@ -211,7 +214,7 @@
         s3(c, keep).wait_send()
 
 
-def front(x_in, gain, w_q, w_k, w_v, cosv, sinv, steps, width_full):
+def front(x_in, gain, w_q, w_k, w_v, steps, width_full):
     rows, width = x_in.shape
     nb = rows // steps
     cols = w_q.shape[1] + 2 * w_k.shape[1]
@@ -221,7 +224,7 @@
     return pl.pallas_call(
         functools.partial(front_body, width_full=width_full),
         out_shape=jax.ShapeDtypeStruct((steps, nb, cols), BF16),
-        in_specs=[vm] * 7,
+        in_specs=[vm] * 5,
         out_specs=vm,
         scratch_shapes=[
             pltpu.VMEM((8, LANE), F32), pltpu.VMEM((3, 8, LANE), F32),
@@ -229,9 +232,9 @@
             pltpu.VMEM((steps, hb, cols), BF16), pltpu.VMEM((steps, hb, cols), BF16), pltpu.VMEM((steps, hb, cols), BF16),
             dma((3,)), dma((3,)), dma((steps,)), dma((steps,)), dma((steps,)), dma((steps,)), dma((steps,)), dma((steps,)),
         ],
-        compiler_params=pltpu.CompilerParams(collective_id=2, has_side_effects=True, vmem_limit_bytes=24 * MIB),
+        compiler_params=pltpu.CompilerParams(collective_id=2, has_side_effects=True, vmem_limit_bytes=60 * MIB),
         cost_estimate=pl.CostEstimate(flops=2 * rows * width * cols, bytes_accessed=4 * MIB, transcendentals=0),
-    )(x_in, gain, w_q, w_k, w_v, cosv, sinv)
+    )(x_in, gain, w_q, w_k, w_v)
 
 
 def tail_body(mix_ref, wo_ref, xin_ref, g_ref, wr_ref, ch_ref, wact_hbm, wlin_hbm, wdn_hbm, out_ref,
@@ -382,6 +385,33 @@
                 hs[rows(k, i * SUB, SUB), q * ff:(q + 1) * ff] = acc[q]
             return carry
         lax.fori_loop(0, ns // SUB, tile, 0)
+        s1(k).start()
+
+    def experts_pick(c, part, k, hd, prior, chs):
+        rounds = 4
+        span, tiles = experts // 2 // rounds, ns // SUB // rounds
+
+        def both(i, carry):
+            for q in range(span):
+                e = part * (experts // 2) + i * span + q
+                hval = jnp.dot(hh[c * nb:(c + 1) * nb, :], wcat[e], preferred_element_type=F32)
+                hd[e] = hval[:, 0:ff].astype(BF16)
+                hd[experts + e] = hval[:, ff:2 * ff].astype(BF16)
+            for q in range(tiles):
+                row = (i * tiles + q) * SUB
+                r = pl.ds(pl.multiple_of((k % per) * ns + row, SUB), SUB)
+                ch = [chs[j, rows(k, row, SUB), :] for j in range(top)]
+                acc = [jnp.zeros((SUB, ff), BF16) for _ in range(2 * top)]
+                for e in range(experts):
+                    va, vl = prior[e, r, :], prior[experts + e, r, :]
+                    for j in range(top):
+                        m = ch[j] == jnp.asarray(e, BF16)
+                        acc[2 * j] = jnp.where(m, va, acc[2 * j])
+                        acc[2 * j + 1] = jnp.where(m, vl, acc[2 * j + 1])
+                for j in range(2 * top):
+                    hs[rows(k, row, SUB), j * ff:(j + 1) * ff] = acc[j]
+            return carry
+        lax.fori_loop(0, rounds, both, 0)
         s1(k).start()
 
     def logits_mid(k):
@@ -465,7 +495,7 @@
         for d in hops:
             ag_send(out_ref, gs, gr, k, d).start()
 
-    def run(hd, ud, chs, us16):
+    def run(hda, hdb, ud, chs, us16):
         w0.start()
         w1.start()
         w2.start()
@@ -487,57 +517,56 @@
         attn_send(2)
         attn_send(3)
         ready(0)
+        attn_send(4)
+        attn_send(5)
         w0.wait()
         w1.wait()
-        experts_in(0, 0, hd)
+        experts_in(0, 0, hda)
         attn_sum(2)
         attn_sum(3)
-        experts_in(0, 1, hd)
+        experts_in(0, 1, hda)
         norm(2)
         norm(3)
-        attn_send(4)
-        attn_send(5)
-        pick(0, hd, chs)
-        pick(1, hd, chs)
+        pick(0, hda, chs)
+        attn_sum(4)
+        attn_sum(5)
+        pick(1, hda, chs)
         part_b(0)
+        norm(4)
+        norm(5)
         part_b(1)
         ready(1)
-        experts_in(1, 0, hd)
-        attn_sum(4)
-        attn_sum(5)
-        experts_in(1, 1, hd)
-        norm(4)
-        norm(5)
+        experts_in(1, 0, hdb)
+        experts_in(1, 1, hdb)
         part_u(0, chs)
-        pick(2, hd, chs)
+        pick(2, hdb, chs)
         part_u(1, chs)
-        pick(3, hd, chs)
         part_b(2)
+        ready(2)
+        experts_pick(2, 0, 3, hda, hdb, chs)
         part_f(0)
         part_b(3)
-        part_f(1)
         w2.wait()
         part_d(0, ud, chs, us16)
-        ready(2)
-        experts_in(2, 0, hd)
+        part_u(2, chs)
+        part_f(1)
+        experts_in(2, 1, hda)
+        pick(4, hda, chs)
+        part_u(3, chs)
+        part_g(0)
         part_d(1, ud, chs, us16)
-        experts_in(2, 1, hd)
-        part_u(2, chs)
-        pick(4, hd, chs)
-        part_u(3, chs)
-        pick(5, hd, chs)
         part_b(4)
+        pick(5, hda, chs)
         part_f(2)
         part_b(5)
-        part_f(3)
-        part_g(0)
         part_d(2, ud, chs, us16)
         part_g(1)
+        part_f(3)
         part_u(4, chs)
         part_d(3, ud, chs, us16)
+        part_g(2)
         part_u(5, chs)
         part_f(4)
-        part_g(2)
         part_d(4, ud, chs, us16)
         part_f(5)
         part_g(3)
@@ -546,7 +575,7 @@
         part_g(5)
 
     bf = functools.partial(pltpu.VMEM, dtype=BF16)
-    pl.run_scoped(run, bf((2 * experts, nb, ff)), bf((ns, experts * ff)), bf((top, steps * nb, ff)), bf((top, ns, ff)))
+    pl.run_scoped(run, bf((2 * experts, nb, ff)), bf((2 * experts, nb, ff)), bf((ns, experts * ff)), bf((top, steps * nb, ff)), bf((top, ns, ff)))
 
     for k in range(parts):
         for i in slots:
@@ -602,14 +631,6 @@
     )(mixed, wo, x_in, gain, w_router, chosen, w_act, w_lin, w_down.reshape(experts * ff, width))
 
 
-def turn_tables(positions, head_dim):
-    half_dim = head_dim // 2
-    inv_freq = ROPE_BASE ** (-(jnp.arange(half_dim, dtype=F32) * 2.0 / head_dim))
-    angles = positions.astype(F32)[:, None] * inv_freq[None, :]
-    cosine, sine_val = jnp.cos(angles), jnp.sin(angles)
-    return jnp.tile(cosine, (1, 4)), jnp.tile(jnp.concatenate([-sine_val, sine_val], axis=1), (1, 2))
-
-
 def solution(mesh):
     x_count = mesh.shape['x']
     cache_spec = P('dp', None, 'y', None)
@@ -624,12 +645,11 @@
         width_full = width * x_count
         group = q_cols // kv_cols
         rows = steps * nb
-        positions = (lengths[None, :] + jnp.arange(steps, dtype=lengths.dtype)[:, None]).reshape(rows)
-        cosv, sinv = turn_tables(positions, hdim)
         x_in = emb_table.at[tokens].get(mode="promise_in_bounds").reshape(rows, width)
-        first = lax.broadcasted_iota(jnp.int32, (2, width), 0) == 0
-        gains = jnp.where(first, g_attn[None, :], g_ffn[None, :]).astype(F32)
-        proj = front(x_in, gains, w_q, w_k, w_v, cosv.reshape(steps, nb, LANE), sinv.reshape(steps, nb, LANE), steps, width_full)
+        line = lax.broadcasted_iota(jnp.int32, (3, width), 0)
+        spread = jnp.pad(lengths.astype(F32), (0, width - nb))
+        gains = jnp.where(line == 0, g_attn.astype(F32)[None, :], jnp.where(line == 1, g_ffn.astype(F32)[None, :], spread[None, :]))
+        proj = front(x_in, gains, w_q, w_k, w_v, steps, width_full)
         kc = k_cache.transpose(0, 2, 3, 1).reshape(nb, kv_cols, seq)
         vc = v_cache.transpose(0, 2, 3, 1).reshape(nb, kv_cols, seq)
         mixed, ko, vo = attention(lengths, proj, kc, vc, group)

time: 157 us -> 150 us (0.955)
  local copies, waits for them, and re-layouts: 12.1 us -> 7.62 us
  Pallas kernels: 141 us -> 138 us
    unnamed x15 -> x1, local copies, waits for them, and re-layouts: 6.17 us -> 1.94 us
    pallas_call x1, Pallas kernels: 87.2 us -> 83 us  [tail(): pl.pallas_call(functools.partial(tail_body, width_full=width_full), out_s...]
    pallas_call x1, Pallas kernels: 21.4 us -> 23.6 us  [front(): pl.pallas_call(functools.partial(front_body, width_full=width_full), out_...]
where the time goes in v4:
time: 150 us
  Pallas kernels  138 us (92%)
  local copies, waits for them, and re-layouts  7.62 us (5%)
  other arithmetic  3.41 us (2%)
    pallas_call x1, Pallas kernels, tail(): pl.pallas_call(functools.partial(tail_body, width_full=width_full), out_s...  83 us
    pallas_call x1, Pallas kernels, attention(): pl.pallas_call(functools.partial(attn_body, group=group), grid_spec=pltpu...  31.2 us
    pallas_call x1, Pallas kernels, front(): pl.pallas_call(functools.partial(front_body, width_full=width_full), out_...  23.6 us
    gather x1, local copies, waits for them, and re-layouts, per_device(): emb_table.at[tokens].get(mode='promise_in_bounds').reshape(rows, width)  5.66 us

profile of v4, /device:TPU:0, one launch (start us, length us, event | category | flops | bytes accessed | tf_op | source)
XLA Modules:
  0.0 149.5 jit_solution(4093071510758981425)
XLA Ops:
  0.6 0.7 convert_element_type.13
  1.3 0.7 convert_element_type.11
  2.0 0.7 convert_element_type.12
  2.7 0.7 select_select_fusion.g_ref
  3.3 0.7 compare_select_fusion
  4.1 5.7 %gather_fusion = bf16[768,384]{1,0:T(8,128)(2,1)} fusion(bf16[49152,384]{1,0:T(8,128)(2,1)} %param.19, s32[1024]{0:T(1024)S(1)} %pad_clamp_fusion), kind=kCustom, calls=%fused_computation | custom fusion | bytes 1182720 | tf_op jit(solution)/shard_map/gather | solution.py:648
  9.7 23.6 %shard_map.175.q_ref.kn_ref.vn_ref = bf16[3,256,640]{2,1,0:T(8,128)(2,1)} custom-call(bf16[768,384]{1,0:T(8,128)(2,1)} %gather_fusion, f32[3,384]{1,0:T(4,128)} %select_select_fusion.g_ref, bf16[384,384]{1,0:T(8,128)(2,1)} %wq_ref.1, bf16[384,128]{1,0:T(8,128)(2,1)} %wk_ref.1, bf16[384,128]{1,0:T(8,128)(2,1)} %wv_ref.1), custom_call_target="tpu_custom_call" | custom-call | flops 377487360 | bytes 4194304 | tf_op jit(solution)/shard_map/pallas_call | solution.py:224
  33.3 31.2 %shard_map.176 = (bf16[3,256,384]{2,1,0:T(8,128)(2,1)}, bf16[256,128,256]{2,1,0:T(8,128)(2,1)}, bf16[256,128,256]{2,1,0:T(8,128)(2,1)}) custom-call(s32[256]{0:T(256)} %len_ref.1, bf16[3,256,640]{2,1,0:T(8,128)(2,1)} %shard_map.175.q_ref.kn_ref.vn_ref, bf16[3,256,640]{2,1,0:T(8,128)(2,1)} %shard_map.175.q_ref.kn_ref.vn_ref, ...), custom_call_target="tpu_custom_call" | custom-call | flops 1073741824 | bytes 67108864 | tf_op jit(solution)/shard_map/pallas_call | solution.py:97
  64.6 83.0 %shard_map.177 = bf16[768,384]{1,0:T(8,128)(2,1)} custom-call(bf16[3,256,384]{2,1,0:T(8,128)(2,1)} %get-tuple-element.6.mix_ref, bf16[384,384]{1,0:T(8,128)(2,1)} %wo_ref.1, bf16[768,384]{1,0:T(8,128)(2,1)} %gather_fusion, f32[3,384]{1,0:T(4,128)} %select_select_fusion.g_ref, bf16[40,384]{1,0:T(8,128)(2,1)} %bitcast.22, s32[3,8,256]{2,1,0:T(8,128)} %bitcast.23, ...), custom_call_target="tpu_custom_call" | custom-call | flops 9059696640 | bytes 12582912 | tf_op jit(solution)/shard_map/pallas_call | solution.py:615
  147.6 1.9 %copy.20 = bf16[3,256,384]{2,1,0:T(8,128)(2,1)} copy(bf16[3,256,384]{2,1,0:T(8,128)(2,1)} %bitcast.18) | data formatting | bytes 1179648
  (4 shorter events, 0.0 us)

commit v5 on v4

--- a/solution.py
+++ b/solution.py
@@ -545,9 +545,9 @@
         ready(2)
         experts_pick(2, 0, 3, hda, hdb, chs)
         part_f(0)
-        part_b(3)
         w2.wait()
         part_d(0, ud, chs, us16)
+        part_b(3)
         part_u(2, chs)
         part_f(1)
         experts_in(2, 1, hda)
@@ -645,7 +645,7 @@
         width_full = width * x_count
         group = q_cols // kv_cols
         rows = steps * nb
-        x_in = emb_table.at[tokens].get(mode="promise_in_bounds").reshape(rows, width)
+        x_in = emb_table.at[tokens].get(mode="promise_in_bounds", wrap_negative_indices=False).reshape(rows, width)
         line = lax.broadcasted_iota(jnp.int32, (3, width), 0)
         spread = jnp.pad(lengths.astype(F32), (0, width - nb))
         gains = jnp.where(line == 0, g_attn.astype(F32)[None, :], jnp.where(line == 1, g_ffn.astype(F32)[None, :], spread[None, :]))

time: 150 us -> 151 us (level)
  no operation moved by 1% of the time
where the time goes in v5:
time: 151 us; the launch traced here: 150 us
  Pallas kernels  139 us (92%)
  local copies, waits for them, and re-layouts  8.3 us (5%)
  other arithmetic  2.72 us (2%)
    pallas_call x1, Pallas kernels, tail(): pl.pallas_call(functools.partial(tail_body, width_full=width_full), out_s...  83.9 us
    pallas_call x1, Pallas kernels, attention(): pl.pallas_call(functools.partial(attn_body, group=group), grid_spec=pltpu...  31.2 us
    pallas_call x1, Pallas kernels, front(): pl.pallas_call(functools.partial(front_body, width_full=width_full), out_...  23.6 us
    gather x1, local copies, waits for them, and re-layouts, per_device(): emb_table.at[tokens]  5.66 us

profile of v5, /device:TPU:0, one launch (start us, length us, event | category | flops | bytes accessed | tf_op | source)
XLA Modules:
  0.0 150.4 jit_solution(2668582970378935854)
XLA Ops:
  0.6 0.7 convert_element_type.13
  1.3 0.7 convert_element_type.11
  2.0 0.7 convert_element_type.12
  2.7 0.7 select_select_fusion.g_ref
  3.3 0.7 reshape.39
  4.1 5.7 %gather_fusion = bf16[768,384]{1,0:T(8,128)(2,1)} fusion(bf16[49152,384]{1,0:T(8,128)(2,1)} %param.19, s32[1024]{0:T(1024)S(1)} %pad_clamp_fusion), kind=kCustom, calls=%fused_computation | custom fusion | bytes 1182720 | tf_op jit(solution)/shard_map/gather | solution.py:648
  9.7 23.6 %shard_map.175.q_ref.kn_ref.vn_ref = bf16[3,256,640]{2,1,0:T(8,128)(2,1)} custom-call(bf16[768,384]{1,0:T(8,128)(2,1)} %gather_fusion, f32[3,384]{1,0:T(4,128)} %select_select_fusion.g_ref, bf16[384,384]{1,0:T(8,128)(2,1)} %wq_ref.1, bf16[384,128]{1,0:T(8,128)(2,1)} %wk_ref.1, bf16[384,128]{1,0:T(8,128)(2,1)} %wv_ref.1), custom_call_target="tpu_custom_call" | custom-call | flops 377487360 | bytes 4194304 | tf_op jit(solution)/shard_map/pallas_call | solution.py:224
  33.3 31.2 %shard_map.176 = (bf16[3,256,384]{2,1,0:T(8,128)(2,1)}, bf16[256,128,256]{2,1,0:T(8,128)(2,1)}, bf16[256,128,256]{2,1,0:T(8,128)(2,1)}) custom-call(s32[256]{0:T(256)} %len_ref.1, bf16[3,256,640]{2,1,0:T(8,128)(2,1)} %shard_map.175.q_ref.kn_ref.vn_ref, bf16[3,256,640]{2,1,0:T(8,128)(2,1)} %shard_map.175.q_ref.kn_ref.vn_ref, ...), custom_call_target="tpu_custom_call" | custom-call | flops 1073741824 | bytes 67108864 | tf_op jit(solution)/shard_map/pallas_call | solution.py:97
  64.6 83.9 %shard_map.177 = bf16[768,384]{1,0:T(8,128)(2,1)} custom-call(bf16[3,256,384]{2,1,0:T(8,128)(2,1)} %get-tuple-element.6.mix_ref, bf16[384,384]{1,0:T(8,128)(2,1)} %wo_ref.1, bf16[768,384]{1,0:T(8,128)(2,1)} %gather_fusion, f32[3,384]{1,0:T(4,128)} %select_select_fusion.g_ref, bf16[40,384]{1,0:T(8,128)(2,1)} %bitcast.22, s32[3,8,256]{2,1,0:T(8,128)} %bitcast.23, ...), custom_call_target="tpu_custom_call" | custom-call | flops 9059696640 | bytes 12582912 | tf_op jit(solution)/shard_map/pallas_call | solution.py:615
  148.5 1.9 %copy.20 = bf16[3,256,384]{2,1,0:T(8,128)(2,1)} copy(bf16[3,256,384]{2,1,0:T(8,128)(2,1)} %bitcast.18) | data formatting | bytes 1179648
  (3 shorter events, 0.0 us)
